TPU v7x, 8 devices: a whole 2x2x1 slice. The times are simulated.
8 devices in a mesh: dp: 2 (over z, y), ep: 4 (over x, core).
Axes of the slice: x: 2, y: 2, z: 1, core: 2. Of those that a mesh axis runs over, the one named last changes fastest.
Arguments:
- tokens: bfloat16 [1024, 1024], P(('dp', 'ep')), parts along dimension 0
- expert_ids: int32 [1024, 8], P(('dp', 'ep')), parts along dimension 0
- gate_vals: float32 [1024, 8], P(('dp', 'ep')), parts along dimension 0
- w_gate: bfloat16 [32, 1024, 512], P('ep')
- w_up: bfloat16 [32, 1024, 512], P('ep')
- w_down: bfloat16 [32, 512, 1024], P('ep')
- grad_out: bfloat16 [1024, 1024], P(('dp', 'ep')), parts along dimension 0
Outputs:
- output 1: bfloat16 [1024, 1024], P(('dp', 'ep')), parts along dimension 0
- output 2: bfloat16 [1024, 1024], P(('dp', 'ep')), parts along dimension 0
- output 3: bfloat16 [64, 1024, 512], P(('dp', 'ep')), parts along dimension 0
- output 4: bfloat16 [64, 1024, 512], P(('dp', 'ep')), parts along dimension 0
- output 5: bfloat16 [64, 512, 1024], P(('dp', 'ep')), parts along dimension 0
There are 2 independent parts. A program takes and returns all parts, laid end to end along the dimension named above; an argument that names none is the same for every part.
All inputs are finite; a program needn't handle non-finite values.
Results may differ from a plain program's by a relative error of at most 0.00104.
Values are sent between devices in bfloat16 or wider.
A program may use at most 1 GiB of HBM per device.

v0:
```python
import functools

import jax
import jax.numpy as jnp
from jax import lax
from jax.experimental import pallas as pl
from jax.experimental.pallas import tpu as pltpu
from jax.sharding import PartitionSpec as P

MESH = pl.DeviceIdType.MESH
F32 = jnp.float32
BF16 = jnp.bfloat16
NT = (((1,), (1,)), ((), ()))
MISS = -4096.0
DC = 256


def chunks(total, size):
    return [slice(i, i + size) for i in range(0, total, size)]


def build_tables(inbox, cols_of, pt, tok, cap, n_loc, s):
    blk = 2 * cap
    g, r = inbox[s, 0], inbox[s, 1] + (s % 2) * cap
    block = jnp.concatenate([g, r, jnp.zeros((128 - 2 * n_loc, tok), F32)], axis=0).T
    rows = slice(s * tok, (s + 1) * tok)
    cols_of[rows, :] = block
    lane = lax.broadcasted_iota(jnp.int32, (tok, blk), 1).astype(F32)
    for e in range(1, n_loc):
        pt[rows, (e - 1) * blk:e * blk] = jnp.where(block[:, n_loc + e:n_loc + e + 1] == lane, 1.0, 0.0).astype(BF16)


def picker(inbox, tok, cap, h, e):
    row = pl.ds(e, 1)
    r = jnp.concatenate([inbox[2 * h, 1, row, :], inbox[2 * h + 1, 1, row, :] + cap], axis=1)
    g = jnp.concatenate([inbox[2 * h, 0, row, :], inbox[2 * h + 1, 0, row, :]], axis=1)
    here = lax.broadcasted_iota(jnp.int32, (2 * cap, 2 * tok), 0).astype(F32) == r
    gate = jnp.sum(jnp.where(here, g, 0.0), axis=1, keepdims=True)
    return jnp.where(here, 1.0, 0.0).astype(BF16), gate


def layer_kernel(n_loc, tok, cap, d, ff, x_hbm, dy_hbm, ids_ref, gates_ref, w1_hbm, w3_hbm, w2_hbm,
                 y_ref, dxo_hbm, dxf_hbm, u0_hbm, da0_hbm, db0_hbm, uc_hbm, dac_hbm, dbc_hbm, xs_hbm, dys_hbm, inbox,
                 w1, w3, w2, c1_0, c2_0, c1_c, c2_c, xb, dyb, xg, doc, do0, y_acc, dx_acc, y_a, y_b, y_c, dx_a, dx_b,
                 meta, cols_of, pt, pg, rc, u0, da0, db0, uc, dac, dbc,
                 w_sem, in_sem, out_sem, send_sem, recv_sem):
    half = 2 * tok
    blk = 2 * cap
    n_exp = 4 * n_loc
    dcols = chunks(d, DC)
    n_ch = len(dcols)
    dp = lax.axis_index("dp")
    me = lax.axis_index("ep")
    chip, core = me // 2, me % 2
    partner = chip * 2 + (1 - core)
    remote = (1 - chip) * 2 + core
    diag = (1 - chip) * 2 + (1 - core)

    def load(i, src, dst, e):
        return pltpu.make_async_copy(src.at[e], dst.at[e], w_sem.at[i, e])

    w_in = [load(i, src, dst, e) for e in range(n_loc) for i, (src, dst) in enumerate(((w1_hbm, w1), (w3_hbm, w3)))]
    w_in += [load(2, w2_hbm, w2, e) for e in range(n_loc)]
    ahead = 6
    waited = [0]

    def wait_w(upto):
        while waited[0] < upto:
            w_in[waited[0]].wait()
            if waited[0] + ahead < len(w_in):
                w_in[waited[0] + ahead].start()
            waited[0] += 1

    sends = []

    def send(src, dst, dev):
        k = len(sends)
        cp = pltpu.make_async_remote_copy(src_ref=src, dst_ref=dst, send_sem=send_sem.at[k], recv_sem=recv_sem.at[k],
                                          device_id=(dp, dev), device_id_type=MESH)
        sends.append(cp)
        return cp

    def slot(buf, s):
        return buf.at[pl.ds(s * tok, tok)]

    outs = []

    def out(src, dst):
        cp = pltpu.make_async_copy(src, dst, out_sem.at[len(outs)])
        cp.start()
        outs.append(cp)

    x_in = pltpu.make_async_copy(x_hbm, slot(xb, 0), in_sem.at[0])
    dy_in = pltpu.make_async_copy(dy_hbm, slot(dyb, 0), in_sem.at[1])
    x_in.start()
    dy_in.start()
    for cp in w_in[:ahead]:
        cp.start()

    expert = lax.broadcasted_iota(jnp.int32, (n_exp, tok), 0)
    gate = jnp.zeros((n_exp, tok), F32)
    hit = jnp.zeros((n_exp, tok), F32)
    for j in range(ids_ref.shape[0]):
        same = expert == ids_ref[j:j + 1, :]
        gate = jnp.where(same, gates_ref[j:j + 1, :], gate)
        hit = jnp.where(same, 1.0, hit)
    before = lax.broadcasted_iota(jnp.int32, (tok, tok), 0) < lax.broadcasted_iota(jnp.int32, (tok, tok), 1)
    rank = jnp.dot(hit.astype(BF16), jnp.where(before, 1.0, 0.0).astype(BF16), preferred_element_type=F32)
    meta[0] = gate
    meta[1] = jnp.where(hit > 0, rank, MISS)

    barrier = pltpu.get_barrier_semaphore()
    for dev in (partner, remote, diag):
        pl.semaphore_signal(barrier, inc=1, device_id=(dp, dev), device_id_type=MESH)
    pl.semaphore_wait(barrier, 3)

    m_snd = [send(meta.at[:, pl.ds(dev * n_loc, n_loc)], inbox.at[k + 1], dev) for k, dev in enumerate((partner, remote, diag))]
    x_snd, dy_snd = [[send(slot(b, 0), slot(b, 1), partner), send(slot(b, 0), slot(b, 2), remote),
                      send(slot(b, 2), slot(b, 3), partner)] for b in (xb, dyb)]
    yb_snd = send(y_acc.at[:, pl.ds(tok, tok)], y_b, partner)
    ya_snd = [send(y_acc.at[c, pl.ds(3 * tok, tok)], y_a.at[c], partner) for c in range(n_ch)]
    yc_snd = [send(y_acc.at[c, pl.ds(2 * tok, tok)], y_c.at[c], remote) for c in range(n_ch)]
    dxa_snd = [send(dx_acc.at[c, pl.ds(3 * tok, tok)], dx_a.at[c], partner) for c in range(n_ch)]
    dxb_snd = [send(dx_acc.at[c, pl.ds(tok, tok)], dx_b.at[c], partner) for c in range(n_ch)]

    for cp in m_snd:
        cp.start()
    x_in.wait()
    x_snd[1].start()
    x_snd[0].start()
    dy_in.wait()
    dy_snd[1].start()
    dy_snd[0].start()

    def pickers(h):
        for e in range(1, n_loc):
            one_hot, gate_row = picker(inbox, tok, cap, h, e)
            pg[h, brows(e), :] = one_hot
            rc[h, brows(e), :] = jnp.broadcast_to(gate_row, (blk, 128))

    def hrows(h):
        return slice(h * half, (h + 1) * half)

    def brows(e):
        return slice((e - 1) * blk, e * blk)

    def gate_col(e, h):
        return cols_of[hrows(h), e:e + 1]

    def gather_x(h):
        for c in dcols:
            xg[:, c] = jnp.dot(pg[h], xb[hrows(h), c], preferred_element_type=F32).astype(BF16)

    def gather_dy(h):
        for e in range(1, n_loc):
            r = brows(e)
            g = jnp.concatenate([rc[h, r, :]] * (DC // 128), axis=1)
            for c in dcols:
                doc[h, r, c] = (g * jnp.dot(pg[h, r, :], dyb[hrows(h), c], preferred_element_type=F32)).astype(BF16)

    def fwd_act(e, h):
        x = xb[hrows(h), :] if e == 0 else xg[brows(e), :]
        for c in chunks(ff, 256):
            a = jnp.dot(x, w1[e, :, c], preferred_element_type=F32)
            b = jnp.dot(x, w3[e, :, c], preferred_element_type=F32)
            if e == 0:
                routed = gate_col(e, h) > 0
                a = jnp.where(routed, a, 0.0)
                b = jnp.where(routed, b, 0.0)
            s = 1.0 / (1.0 + jnp.exp(-a))
            s_a = a * s
            p1 = b * (s + s_a * (1.0 - s))
            u = (s_a * b).astype(BF16)
            if e == 0:
                c1_0[hrows(h), c], c2_0[hrows(h), c], u0[hrows(h), c] = p1, s_a, u
            else:
                c1_c[h, brows(e), c], c2_c[h, brows(e), c], uc[h, brows(e), c] = p1, s_a, u

    def fwd_out(e, h, k):
        u = u0[hrows(h), :] if e == 0 else uc[h, brows(e), :]
        g = gate_col(e, h)
        o = jnp.dot(u, w2[e, :, dcols[k]], preferred_element_type=F32).astype(BF16)
        if e == 0:
            y_acc[k, hrows(h), :] = g * o.astype(F32)
        else:
            y_acc[k, hrows(h), :] += g * jnp.dot(pt[hrows(h), brows(e)], o, preferred_element_type=F32)

    def bwd_act_dense(h):
        g = gate_col(0, h)
        for c in dcols:
            do0[:, c] = (g * dyb[hrows(h), c].astype(F32)).astype(BF16)
        do = do0[...]
        for c in chunks(ff, 256):
            du = lax.dot_general(do, w2[0, c, :], NT, preferred_element_type=F32)
            da0[hrows(h), c] = (du * c1_0[hrows(h), c]).astype(BF16)
            db0[hrows(h), c] = (du * c2_0[hrows(h), c]).astype(BF16)

    def bwd_act(e):
        r = brows(e)
        do = jnp.concatenate([doc[0, r, :], doc[1, r, :]], axis=0)
        for c in chunks(ff, 256):
            du = lax.dot_general(do, w2[e, c, :], NT, preferred_element_type=F32)
            for h in range(2):
                part = du[h * blk:(h + 1) * blk, :]
                dac[h, r, c] = (part * c1_c[h, r, c]).astype(BF16)
                dbc[h, r, c] = (part * c2_c[h, r, c]).astype(BF16)

    def bwd_in(e, k):
        c = dcols[k]
        if e == 0:
            da, db = da0[...], db0[...]
        else:
            da, db = [jnp.concatenate([b[0, brows(e), :], b[1, brows(e), :]], axis=0) for b in (dac, dbc)]
        dx = (lax.dot_general(da, w1[e, c, :], NT, preferred_element_type=F32)
              + lax.dot_general(db, w3[e, c, :], NT, preferred_element_type=F32)).astype(BF16)
        if e == 0:
            dx_acc[k] = dx.astype(F32)
        else:
            for h in range(2):
                doc[h, brows(e), c] = dx[h * blk:(h + 1) * blk, :]

    def scatter_dx(h, k):
        dx_acc[k, hrows(h), :] += jnp.dot(pt[hrows(h), :], doc[h, :, dcols[k]], preferred_element_type=F32)

    def relay(snd):
        snd[1].wait_recv()
        snd[2].start()

    def forward_y(k):
        ya_snd[k].wait_recv()
        y_acc[k, 2 * tok:3 * tok, :] += y_a[k]
        yc_snd[k].start()

    def finish_dx(k):
        dxa_snd[k].wait_recv()
        dx_acc[k, 2 * tok:3 * tok, :] += dx_a[k]
        out(dx_acc.at[k, pl.ds(2 * tok, tok)], dxf_hbm.at[:, pl.ds(k * DC, DC)])
        dxb_snd[k].wait_recv()
        dx_acc[k, 0:tok, :] += dx_b[k]
        out(dx_acc.at[k, pl.ds(0, tok)], dxo_hbm.at[:, pl.ds(k * DC, DC)])

    inbox[0] = meta[:, pl.ds(me * n_loc, n_loc), :]
    build_tables(inbox, cols_of, pt, tok, cap, n_loc, 0)
    for cp in m_snd:
        cp.wait_recv()
    build_tables(inbox, cols_of, pt, tok, cap, n_loc, 1)
    pickers(0)
    x_snd[0].wait_recv()
    gather_x(0)
    for s in (2, 3):
        build_tables(inbox, cols_of, pt, tok, cap, n_loc, s)
    pickers(1)
    for e in range(n_loc):
        wait_w(2 * e + 2)
        fwd_act(e, 0)
    dy_snd[0].wait_recv()
    for e in range(n_loc):
        wait_w(2 * n_loc + e + 1)
        if e == n_loc - 2:
            relay(x_snd)
        for k in range(n_ch):
            fwd_out(e, 0, k)
    yb_snd.start()
    gather_dy(0)
    bwd_act_dense(0)

    x_snd[2].wait_recv()
    out(xb, xs_hbm)
    gather_x(1)
    for e in range(n_loc):
        fwd_act(e, 1)
    out(uc, uc_hbm)
    out(u0, u0_hbm)
    for k in range(n_ch):
        for e in range(n_loc):
            fwd_out(e, 1, k)
        ya_snd[k].start()
        if k == 1:
            relay(dy_snd)
        if k >= 2:
            forward_y(k - 2)

    dy_snd[2].wait_recv()
    out(dyb, dys_hbm)
    bwd_act_dense(1)
    out(da0, da0_hbm)
    out(db0, db0_hbm)
    forward_y(n_ch - 2)
    gather_dy(1)
    forward_y(n_ch - 1)
    for e in range(1, n_loc):
        bwd_act(e)
    out(dac, dac_hbm)
    out(dbc, dbc_hbm)
    for k in range(n_ch):
        for e in range(n_loc):
            bwd_in(e, k)
        scatter_dx(1, k)
        dxa_snd[k].start()
        scatter_dx(0, k)
        dxb_snd[k].start()
        if k >= 1:
            finish_dx(k - 1)
    yb_snd.wait_recv()
    for k in range(n_ch):
        yc_snd[k].wait_recv()
        y_ref[:, dcols[k]] = (y_acc[k, 0:tok, :] + y_b[k] + y_c[k]).astype(BF16)
    finish_dx(n_ch - 1)
    for cp in sends:
        cp.wait_send()
    for cp in outs:
        cp.wait()


def layer_call(x, dy, ids, gates, w1, w3, w2, cap):
    tok, d = x.shape
    n_loc, _, ff = w1.shape
    rows = 4 * tok
    cold = (n_loc - 1) * 2 * cap
    n_ch = d // DC
    any_spec = pl.BlockSpec(memory_space=pl.ANY)
    vmem_spec = pl.BlockSpec(memory_space=pltpu.VMEM)
    sds = jax.ShapeDtypeStruct
    vm = pltpu.VMEM
    n_send = 3 + 6 + 1 + 4 * n_ch
    return pl.pallas_call(
        functools.partial(layer_kernel, n_loc, tok, cap, d, ff),
        out_shape=(sds((tok, d), BF16), sds((tok, d), F32), sds((tok, d), F32),
                   sds((rows, ff), BF16), sds((rows, ff), BF16), sds((rows, ff), BF16),
                   sds((2, cold, ff), BF16), sds((2, cold, ff), BF16), sds((2, cold, ff), BF16),
                   sds((rows, d), BF16), sds((rows, d), BF16), sds((4, 2, n_loc, tok), F32)),
        in_specs=[any_spec, any_spec, vmem_spec, vmem_spec, any_spec, any_spec, any_spec],
        out_specs=(vmem_spec,) + (any_spec,) * 10 + (vmem_spec,),
        scratch_shapes=[
            vm((n_loc, d, ff), BF16), vm((n_loc, d, ff), BF16), vm((n_loc, ff, d), BF16),
            vm((rows, ff), F32), vm((rows, ff), F32), vm((2, cold, ff), F32), vm((2, cold, ff), F32),
            vm((rows, d), BF16), vm((rows, d), BF16), vm((cold, d), BF16), vm((2, cold, d), BF16), vm((2 * tok, d), BF16),
            vm((n_ch, rows, DC), F32), vm((n_ch, rows, DC), F32),
            vm((n_ch, tok, DC), F32), vm((n_ch, tok, DC), F32), vm((n_ch, tok, DC), F32),
            vm((n_ch, tok, DC), F32), vm((n_ch, tok, DC), F32),
            vm((2, 4 * n_loc, tok), F32), vm((rows, 128), F32),
            vm((rows, cold), BF16), vm((2, cold, 2 * tok), BF16), vm((2, cold, 128), F32),
            vm((rows, ff), BF16), vm((rows, ff), BF16), vm((rows, ff), BF16),
            vm((2, cold, ff), BF16), vm((2, cold, ff), BF16), vm((2, cold, ff), BF16),
            pltpu.SemaphoreType.DMA((3, n_loc)), pltpu.SemaphoreType.DMA((2,)), pltpu.SemaphoreType.DMA((8 + 2 * n_ch,)),
            pltpu.SemaphoreType.DMA((n_send,)), pltpu.SemaphoreType.DMA((n_send,)),
        ],
        compiler_params=pltpu.CompilerParams(collective_id=0, has_side_effects=True, vmem_limit_bytes=67_000_000),
        cost_estimate=pl.CostEstimate(flops=2 * rows * d * ff * n_loc * 4, bytes_accessed=36 << 20, transcendentals=0),
        name="moe_layer",
    )(x, dy, ids, gates, w1, w3, w2)


def grad_kernel(n_loc, tok, cap, d, ff, u0_hbm, da0_hbm, db0_hbm, uc_hbm, dac_hbm, dbc_hbm, xs_hbm, dys_hbm, inbox, y_in,
                gw1_hbm, gw3_hbm, gw2_hbm, y_out, u0, da0, db0, uc, dac, dbc, xs, dys,
                xt_a, do_a, ut_a, xt_b, do_b, ut_b, xt0, do0, g1, g3, g2, in_sem, act_sem, out_sem):
    blk = 2 * cap
    x_in = pltpu.make_async_copy(xs_hbm, xs, in_sem.at[0])
    dy_in = pltpu.make_async_copy(dys_hbm, dys, in_sem.at[1])
    dense_in = [pltpu.make_async_copy(src, dst, in_sem.at[2 + j])
                for j, (src, dst) in enumerate(((da0_hbm, da0), (db0_hbm, db0), (u0_hbm, u0)))]

    def rows_of(e):
        return pl.ds(pl.multiple_of((e - 1) * blk, blk), blk)

    def act_in(e):
        return [pltpu.make_async_copy(src.at[:, rows_of(e)], dst.at[:, rows_of(e)], act_sem.at[j, e])
                for j, (src, dst) in enumerate(((dac_hbm, dac), (dbc_hbm, dbc), (uc_hbm, uc)))]

    def each(copies, act):
        for cp in copies:
            getattr(cp, act)()

    x_in.start()
    each(act_in(1), "start")
    dy_in.start()
    each(act_in(2), "start")
    each(act_in(3), "start")
    y_out[...] = y_in[...]

    def prepare(e, xt, do, ut):
        each(act_in(e), "wait")
        for h in range(2):
            hr = slice(h * 2 * tok, (h + 1) * 2 * tok)
            br = slice(h * blk, (h + 1) * blk)
            one_hot, gate = picker(inbox, tok, cap, h, e)
            for c in chunks(d, 256):
                x = jnp.dot(one_hot, xs[hr, c], preferred_element_type=F32).astype(BF16)
                xt[c, br] = x.T
                do[br, c] = (gate * jnp.dot(one_hot, dys[hr, c], preferred_element_type=F32)).astype(BF16)
            ut[:, br] = uc[h, rows_of(e), :].T

    def out(s, e):
        return [pltpu.make_async_copy(buf.at[s], dst.at[e], out_sem.at[s, j])
                for j, (buf, dst) in enumerate(((g1, gw1_hbm), (g3, gw3_hbm), (g2, gw2_hbm)))]

    def grads(s, e, x_t, u_t, do_e, da, db):
        copies = out(s, e)
        for cp, buf, lhs, rhs in zip(copies, (g1, g3, g2), (x_t, x_t, u_t), (da, db, do_e)):
            for c in chunks(rhs.shape[1], 256):
                buf[s, :, c] = jnp.dot(lhs, rhs[:, c], preferred_element_type=F32).astype(BF16)
            cp.start()

    def cold(s, e, xt, do, ut):
        da, db = [jnp.concatenate([a[0, rows_of(e), :], a[1, rows_of(e), :]], axis=0) for a in (dac, dbc)]
        grads(s, e, xt[...], ut[...], do[...], da, db)

    buf_a, buf_b = (xt_a, do_a, ut_a), (xt_b, do_b, ut_b)
    x_in.wait()
    dy_in.wait()
    prepare(1, *buf_a)

    def pair(j, carry):
        e = 2 * j + 1

        @pl.when(j < 2)
        def _():
            each(act_in(e + 3), "start")
            each(act_in(e + 4), "start")

        @pl.when(j == 2)
        def _():
            each(dense_in, "start")

        @pl.when(j > 0)
        def _():
            each(out(0, e), "wait")

        prepare(e + 1, *buf_b)
        cold(0, e, *buf_a)

        @pl.when(j > 0)
        def _():
            each(out(1, e), "wait")

        prepare(e + 2, *buf_a)
        cold(1, e + 1, *buf_b)
        return carry

    lax.fori_loop(0, (n_loc - 2) // 2, pair, 0)
    each(dense_in, "wait")
    each(out(0, 0), "wait")
    for s in range(4):
        r = slice(s * tok, (s + 1) * tok)
        g = jnp.broadcast_to(inbox[s, 0, 0:1, :], (128, tok)).T
        do0[r, :] = (jnp.concatenate([g] * (d // 128), axis=1) * dys[r, :].astype(F32)).astype(BF16)
    xt0[...] = xs[...].T
    cold(0, n_loc - 1, *buf_a)
    each(out(1, 0), "wait")
    grads(1, 0, xt0[...], u0[...].T, do0[...], da0[...], db0[...])
    each(out(0, 0), "wait")
    each(out(1, 0), "wait")


def grad_call(u0, da0, db0, uc, dac, dbc, xs, dys, inbox, y, n_loc, cap):
    rows, ff = u0.shape
    d = xs.shape[1]
    tok = y.shape[0]
    cold = uc.shape[1]
    sds = jax.ShapeDtypeStruct
    vm = pltpu.VMEM
    any_spec = pl.BlockSpec(memory_space=pl.ANY)
    vmem_spec = pl.BlockSpec(memory_space=pltpu.VMEM)
    act, cact = vm((rows, ff), BF16), vm((2, cold, ff), BF16)
    return pl.pallas_call(
        functools.partial(grad_kernel, n_loc, tok, cap, d, ff),
        out_shape=(sds((n_loc, d, ff), BF16), sds((n_loc, d, ff), BF16), sds((n_loc, ff, d), BF16), sds((tok, d), BF16)),
        in_specs=[any_spec] * 8 + [vmem_spec] * 2,
        out_specs=(any_spec, any_spec, any_spec, vmem_spec),
        scratch_shapes=[act, act, act, cact, cact, cact, vm((rows, d), BF16), vm((rows, d), BF16)]
        + [vm((d, 4 * cap), BF16), vm((4 * cap, d), BF16), vm((ff, 4 * cap), BF16)] * 2
        + [vm((d, rows), BF16), vm((rows, d), BF16), vm((2, d, ff), BF16), vm((2, d, ff), BF16), vm((2, ff, d), BF16),
           pltpu.SemaphoreType.DMA((5,)), pltpu.SemaphoreType.DMA((3, n_loc)), pltpu.SemaphoreType.DMA((2, 3))],
        compiler_params=pltpu.CompilerParams(vmem_limit_bytes=60_000_000),
        cost_estimate=pl.CostEstimate(flops=2 * rows * d * ff * n_loc * 2, bytes_accessed=34 << 20, transcendentals=0),
        name="moe_grads",
    )(u0, da0, db0, uc, dac, dbc, xs, dys, inbox, y)


def solution(mesh):
    group_size = mesh.shape["ep"]
    num_chips = mesh.shape["dp"] * group_size
    tok_spec = P(("dp", "ep"), None)
    w_spec = P("ep", None, None)
    grad_spec = P(("dp", "ep"), None, None)

    def layer_fn(tokens, expert_ids, gate_vals, w_gate, w_up, w_down, grad_out):
        num_experts = w_gate.shape[0]
        n_loc = num_experts // group_size
        tok_dev = tokens.shape[0] // num_chips
        cap = ((2 * tok_dev * expert_ids.shape[1] + 8 * num_experts - 1) // (8 * num_experts)) * 8
        assert group_size == 4 and (num_experts // 2) % n_loc == 0 and n_loc == 8 and tok_dev == 2 * cap == 128

        def device_fn(x, ids, gates, w1, w3, w2, dy):
            y, dx_own, dx_fwd, *saved = layer_call(x, dy, ids.T, gates.T, w1, w3, w2, cap)
            dx_in = lax.ppermute(dx_fwd, "ep", [(0, 2), (1, 3), (2, 0), (3, 1)])
            gw1, gw3, gw2, y = grad_call(*saved, y, n_loc, cap)
            return y, (dx_own + dx_in).astype(BF16), gw1, gw3, gw2

        return jax.shard_map(device_fn, mesh=mesh, in_specs=(tok_spec, tok_spec, tok_spec, w_spec, w_spec, w_spec, tok_spec),
                             out_specs=(tok_spec, tok_spec, grad_spec, grad_spec, grad_spec), check_vma=False)(
                                 tokens, expert_ids, gate_vals, w_gate, w_up, w_down, grad_out)

    return layer_fn
```

profile of v0, /device:TPU:0, one launch (start us, length us, event | category | flops | bytes accessed | tf_op | source)
XLA Modules:
  0.0 59.7 jit_solution(5833235882495865805)
XLA Ops:
  0.6 40.2 %moe_layer.1 = (bf16[128,1024]{1,0:T(8,128)(2,1)}, f32[128,1024]{1,0:T(8,128)}, f32[128,1024]{1,0:T(8,128)}, bf16[512,512]{1,0:T(8,128)(2,1)}, bf16[512,512]{1,0...) custom-call(bf16[128,1024]{1,0:T(8,128)(2,1)} %x_hbm.1, ...), custom_call_target="tpu_custom_call" | custom-call | flops 17179869184 | bytes 37748736 | tf_op jit(solution)/shard_map/moe_layer/pallas_call | solution.py:326
  40.8 1.6 %collective-permute-start = (f32[128,1024]{1,0:T(8,128)}, f32[128,1024]{1,0:T(8,128)S(1)}, u32[]{:S(2)}, u32[]{:S(2)}) collective-permute-start(f32[128,1024]{1,0:T(8,128)} %get-tuple-element.33), channel_id=1, source_target_pairs={{0,2},{1,3},{2,0},{3,1},{4,6},{5,7},{6,4},{7,5}} | collective-permute-start | bytes 1572872 | tf_op jit(solution)/shard_map/ppermute | solution.py:496
  42.4 0.0 copy-start
  42.4 16.5 %moe_grads.1 = (bf16[8,1024,512]{2,1,0:T(8,128)(2,1)}, bf16[8,1024,512]{2,1,0:T(8,128)(2,1)}, bf16[8,512,1024]{2,1,0:T(8,128)(2,1)}, bf16[128,1024]{1,0:T(8,128)(2,1)}) custom-call(bf16[512,512]{1,0:T(8,128)(2,1)} %get-tuple-element.21.u0_hbm, bf16[512,512]{1,0:T(8,128)(2,1)} %get-tuple-element.22.da0_hbm, bf16[512,512]{1,0:T(8,128)(2,1)} %get-tuple-element.23.db0_hbm, ...), custom_call_target="tpu_custom_call" | custom-call | flops 8589934592 | bytes 35651584 | tf_op jit(solution)/shard_map/moe_grads/pallas_call | solution.py:465
  58.9 0.0 collective-permute-done
  58.9 0.0 copy-done
  58.9 0.8 %add_convert_fusion = bf16[128,1024]{1,0:T(8,128)(2,1)} fusion(f32[128,1024]{1,0:T(8,128)S(1)} %copy-done, f32[128,1024]{1,0:T(8,128)S(1)} %collective-permute-done), kind=kLoop, calls=%fused_computation | loop fusion | flops 262144 | bytes 1310720 | tf_op jit(solution)/shard_map/convert_element_type | solution.py:498
Async XLA Ops:
  40.8 18.1 %collective-permute-start = (f32[128,1024]{1,0:T(8,128)}, f32[128,1024]{1,0:T(8,128)S(1)}, u32[]{:S(2)}, u32[]{:S(2)}) collective-permute-start(f32[128,1024]{1,0:T(8,128)} %get-tuple-element.33), channel_id=1, source_target_pairs={{0,2},{1,3},{2,0},{3,1},{4,6},{5,7},{6,4},{7,5}} | collective-permute-start | bytes 1572872 | tf_op jit(solution)/shard_map/ppermute | solution.py:496
  42.4 16.5 %copy-start = (f32[128,1024]{1,0:T(8,128)S(1)}, f32[128,1024]{1,0:T(8,128)}, u32[]{:S(2)}) copy-start(f32[128,1024]{1,0:T(8,128)} %get-tuple-element.32) | copy-start | bytes 1572868
where the time goes:
time: 59.8 us; the launch traced here: 59.7 us
  Pallas kernels  56.7 us (95%)
  starting transfers between devices  1.57 us (3%)
  other arithmetic  0.76 us (1%)
  between operations  0.67 us (1%)
    pallas_call x1, Pallas kernels, layer_call(): pl.pallas_call(functools.partial(layer_kernel, n_loc, tok, cap, d, ff), o...  40.2 us
    pallas_call x1, Pallas kernels, grad_call(): pl.pallas_call(functools.partial(grad_kernel, n_loc, tok, cap, d, ff), ou...  16.5 us
    ppermute x1, starting transfers between devices, device_fn(): dx_in = lax.ppermute(dx_fwd, 'ep', [(0, 2), (1, 3), (2, 0), (3, 1)])  1.57 us
  transfers between devices with their start and end apart: 1, of which 0 were waited for; matrix products, arithmetic and copies ran while one was open for 0% of the time, Pallas kernels for 28%

commit v1 on v0

--- a/solution.py
+++ b/solution.py
@@ -13,6 +13,7 @@
 NT = (((1,), (1,)), ((), ()))
 MISS = -4096.0
 DC = 256
+Y_SHARE = 6
 
 
 def chunks(total, size):
@@ -39,16 +40,15 @@
     return jnp.where(here, 1.0, 0.0).astype(BF16), gate
 
 
-def layer_kernel(n_loc, tok, cap, d, ff, x_hbm, dy_hbm, ids_ref, gates_ref, w1_hbm, w3_hbm, w2_hbm,
-                 y_ref, dxo_hbm, dxf_hbm, u0_hbm, da0_hbm, db0_hbm, uc_hbm, dac_hbm, dbc_hbm, xs_hbm, dys_hbm, inbox,
+def layer_kernel(n_loc, tok, cap, d, ff, y_rows, x_hbm, dy_hbm, ids_ref, gates_ref, w1_hbm, w3_hbm, w2_hbm,
+                 y_ref, dxo_hbm, fwd_hbm, u0_hbm, da0_hbm, db0_hbm, uc_hbm, dac_hbm, dbc_hbm, xs_hbm, dys_hbm, inbox,
                  w1, w3, w2, c1_0, c2_0, c1_c, c2_c, xb, dyb, xg, doc, do0, y_acc, dx_acc, y_a, y_b, y_c, dx_a, dx_b,
-                 meta, cols_of, pt, pg, rc, u0, da0, db0, uc, dac, dbc,
+                 meta, cols_of, pt, pg, rc, u_last, u0, da0, db0, uc, dac, dbc,
                  w_sem, in_sem, out_sem, send_sem, recv_sem):
     half = 2 * tok
     blk = 2 * cap
     n_exp = 4 * n_loc
     dcols = chunks(d, DC)
-    n_ch = len(dcols)
     dp = lax.axis_index("dp")
     me = lax.axis_index("ep")
     chip, core = me // 2, me % 2
@@ -59,17 +59,8 @@
     def load(i, src, dst, e):
         return pltpu.make_async_copy(src.at[e], dst.at[e], w_sem.at[i, e])
 
-    w_in = [load(i, src, dst, e) for e in range(n_loc) for i, (src, dst) in enumerate(((w1_hbm, w1), (w3_hbm, w3)))]
-    w_in += [load(2, w2_hbm, w2, e) for e in range(n_loc)]
-    ahead = 6
-    waited = [0]
-
-    def wait_w(upto):
-        while waited[0] < upto:
-            w_in[waited[0]].wait()
-            if waited[0] + ahead < len(w_in):
-                w_in[waited[0] + ahead].start()
-            waited[0] += 1
+    def load_w(e):
+        return [load(i, src, dst, e) for i, (src, dst) in enumerate(((w1_hbm, w1), (w3_hbm, w3), (w2_hbm, w2)))]
 
     sends = []
 
@@ -94,8 +85,9 @@
     dy_in = pltpu.make_async_copy(dy_hbm, slot(dyb, 0), in_sem.at[1])
     x_in.start()
     dy_in.start()
-    for cp in w_in[:ahead]:
-        cp.start()
+    for e in range(3):
+        for cp in load_w(e):
+            cp.start()
 
     expert = lax.broadcasted_iota(jnp.int32, (n_exp, tok), 0)
     gate = jnp.zeros((n_exp, tok), F32)
@@ -117,11 +109,8 @@
     m_snd = [send(meta.at[:, pl.ds(dev * n_loc, n_loc)], inbox.at[k + 1], dev) for k, dev in enumerate((partner, remote, diag))]
     x_snd, dy_snd = [[send(slot(b, 0), slot(b, 1), partner), send(slot(b, 0), slot(b, 2), remote),
                       send(slot(b, 2), slot(b, 3), partner)] for b in (xb, dyb)]
-    yb_snd = send(y_acc.at[:, pl.ds(tok, tok)], y_b, partner)
-    ya_snd = [send(y_acc.at[c, pl.ds(3 * tok, tok)], y_a.at[c], partner) for c in range(n_ch)]
-    yc_snd = [send(y_acc.at[c, pl.ds(2 * tok, tok)], y_c.at[c], remote) for c in range(n_ch)]
-    dxa_snd = [send(dx_acc.at[c, pl.ds(3 * tok, tok)], dx_a.at[c], partner) for c in range(n_ch)]
-    dxb_snd = [send(dx_acc.at[c, pl.ds(tok, tok)], dx_b.at[c], partner) for c in range(n_ch)]
+    yb_snd, ya_snd, yc_snd = send(slot(y_acc, 1), y_b, partner), send(slot(y_acc, 3), y_a, partner), send(y_acc.at[pl.ds(2 * tok, y_rows)], y_c, remote)
+    dxa_snd, dxb_snd = send(slot(dx_acc, 3), dx_a, partner), send(slot(dx_acc, 1), dx_b, partner)
 
     for cp in m_snd:
         cp.start()
@@ -141,11 +130,19 @@
     def hrows(h):
         return slice(h * half, (h + 1) * half)
 
+    def srows(s):
+        return slice(s * tok, (s + 1) * tok)
+
     def brows(e):
-        return slice((e - 1) * blk, e * blk)
+        if isinstance(e, int):
+            return slice((e - 1) * blk, e * blk)
+        return pl.ds(pl.multiple_of((e - 1) * blk, blk), blk)
 
     def gate_col(e, h):
-        return cols_of[hrows(h), e:e + 1]
+        if isinstance(e, int):
+            return cols_of[hrows(h), e:e + 1]
+        lane = lax.broadcasted_iota(jnp.int32, (half, 128), 1)
+        return jnp.sum(jnp.where(lane == e, cols_of[hrows(h), :], 0.0), axis=1, keepdims=True)
 
     def gather_x(h):
         for c in dcols:
@@ -159,11 +156,12 @@
                 doc[h, r, c] = (g * jnp.dot(pg[h, r, :], dyb[hrows(h), c], preferred_element_type=F32)).astype(BF16)
 
     def fwd_act(e, h):
-        x = xb[hrows(h), :] if e == 0 else xg[brows(e), :]
+        dense = isinstance(e, int) and e == 0
+        x = xb[hrows(h), :] if dense else xg[brows(e), :]
         for c in chunks(ff, 256):
             a = jnp.dot(x, w1[e, :, c], preferred_element_type=F32)
             b = jnp.dot(x, w3[e, :, c], preferred_element_type=F32)
-            if e == 0:
+            if dense:
                 routed = gate_col(e, h) > 0
                 a = jnp.where(routed, a, 0.0)
                 b = jnp.where(routed, b, 0.0)
@@ -171,19 +169,23 @@
             s_a = a * s
             p1 = b * (s + s_a * (1.0 - s))
             u = (s_a * b).astype(BF16)
-            if e == 0:
+            if dense:
                 c1_0[hrows(h), c], c2_0[hrows(h), c], u0[hrows(h), c] = p1, s_a, u
             else:
                 c1_c[h, brows(e), c], c2_c[h, brows(e), c], uc[h, brows(e), c] = p1, s_a, u
-
-    def fwd_out(e, h, k):
-        u = u0[hrows(h), :] if e == 0 else uc[h, brows(e), :]
+                if h == 0:
+                    u_last[:, c] = u
+
+    def fwd_out(e, h):
+        dense = isinstance(e, int) and e == 0
+        u = u0[hrows(h), :] if dense else u_last[...] if h == 0 else uc[h, brows(e), :]
         g = gate_col(e, h)
-        o = jnp.dot(u, w2[e, :, dcols[k]], preferred_element_type=F32).astype(BF16)
-        if e == 0:
-            y_acc[k, hrows(h), :] = g * o.astype(F32)
-        else:
-            y_acc[k, hrows(h), :] += g * jnp.dot(pt[hrows(h), brows(e)], o, preferred_element_type=F32)
+        for c in dcols:
+            o = jnp.dot(u, w2[e, :, c], preferred_element_type=F32).astype(BF16)
+            if dense:
+                y_acc[hrows(h), c] = g * o.astype(F32)
+            else:
+                y_acc[hrows(h), c] += g * jnp.dot(pt[hrows(h), brows(e)], o, preferred_element_type=F32)
 
     def bwd_act_dense(h):
         g = gate_col(0, h)
@@ -205,107 +207,124 @@
                 dac[h, r, c] = (part * c1_c[h, r, c]).astype(BF16)
                 dbc[h, r, c] = (part * c2_c[h, r, c]).astype(BF16)
 
-    def bwd_in(e, k):
-        c = dcols[k]
-        if e == 0:
-            da, db = da0[...], db0[...]
-        else:
-            da, db = [jnp.concatenate([b[0, brows(e), :], b[1, brows(e), :]], axis=0) for b in (dac, dbc)]
-        dx = (lax.dot_general(da, w1[e, c, :], NT, preferred_element_type=F32)
-              + lax.dot_general(db, w3[e, c, :], NT, preferred_element_type=F32)).astype(BF16)
-        if e == 0:
-            dx_acc[k] = dx.astype(F32)
-        else:
+    def bwd_in(e):
+        da, db = [jnp.concatenate([b[0, brows(e), :], b[1, brows(e), :]], axis=0) for b in (dac, dbc)]
+        for c in dcols:
+            dx = (lax.dot_general(da, w1[e, c, :], NT, preferred_element_type=F32)
+                  + lax.dot_general(db, w3[e, c, :], NT, preferred_element_type=F32)).astype(BF16)
             for h in range(2):
                 doc[h, brows(e), c] = dx[h * blk:(h + 1) * blk, :]
 
-    def scatter_dx(h, k):
-        dx_acc[k, hrows(h), :] += jnp.dot(pt[hrows(h), :], doc[h, :, dcols[k]], preferred_element_type=F32)
+    def bwd_in_dense(s0, s1):
+        da, db = [jnp.concatenate([b[srows(s0), :], b[srows(s1), :]], axis=0) for b in (da0, db0)]
+        for c in dcols:
+            dx = (lax.dot_general(da, w1[0, c, :], NT, preferred_element_type=F32)
+                  + lax.dot_general(db, w3[0, c, :], NT, preferred_element_type=F32)).astype(BF16).astype(F32)
+            dx_acc[srows(s0), c] = dx[0:tok, :]
+            dx_acc[srows(s1), c] = dx[tok:, :]
+
+    def scatter_dx(s):
+        for c in dcols:
+            dx_acc[srows(s), c] += jnp.dot(pt[srows(s), :], doc[s // 2, :, c], preferred_element_type=F32)
 
     def relay(snd):
         snd[1].wait_recv()
         snd[2].start()
-
-    def forward_y(k):
-        ya_snd[k].wait_recv()
-        y_acc[k, 2 * tok:3 * tok, :] += y_a[k]
-        yc_snd[k].start()
-
-    def finish_dx(k):
-        dxa_snd[k].wait_recv()
-        dx_acc[k, 2 * tok:3 * tok, :] += dx_a[k]
-        out(dx_acc.at[k, pl.ds(2 * tok, tok)], dxf_hbm.at[:, pl.ds(k * DC, DC)])
-        dxb_snd[k].wait_recv()
-        dx_acc[k, 0:tok, :] += dx_b[k]
-        out(dx_acc.at[k, pl.ds(0, tok)], dxo_hbm.at[:, pl.ds(k * DC, DC)])
 
     inbox[0] = meta[:, pl.ds(me * n_loc, n_loc), :]
     build_tables(inbox, cols_of, pt, tok, cap, n_loc, 0)
     for cp in m_snd:
         cp.wait_recv()
+    x_snd[0].wait_recv()
+    for e in range(2):
+        for cp in load_w(e):
+            cp.wait()
+        for cp in load_w(e + 3):
+            cp.start()
     build_tables(inbox, cols_of, pt, tok, cap, n_loc, 1)
+    fwd_act(0, 0)
     pickers(0)
-    x_snd[0].wait_recv()
     gather_x(0)
     for s in (2, 3):
         build_tables(inbox, cols_of, pt, tok, cap, n_loc, s)
     pickers(1)
-    for e in range(n_loc):
-        wait_w(2 * e + 2)
+    fwd_act(1, 0)
+    fwd_out(0, 0)
+
+    def own(e, carry):
+        for cp in load_w(e):
+            cp.wait()
+
+        @pl.when(e + 3 < n_loc)
+        def _():
+            for cp in load_w(e + 3):
+                cp.start()
+
+        @pl.when(e == n_loc - 1)
+        def _():
+            relay(x_snd)
+
+        fwd_out(e - 1, 0)
         fwd_act(e, 0)
+        return carry
+
+    lax.fori_loop(2, n_loc, own, 0)
     dy_snd[0].wait_recv()
-    for e in range(n_loc):
-        wait_w(2 * n_loc + e + 1)
-        if e == n_loc - 2:
-            relay(x_snd)
-        for k in range(n_ch):
-            fwd_out(e, 0, k)
+    fwd_out(n_loc - 1, 0)
+    gather_dy(0)
     yb_snd.start()
-    gather_dy(0)
     bwd_act_dense(0)
 
     x_snd[2].wait_recv()
     out(xb, xs_hbm)
     gather_x(1)
-    for e in range(n_loc):
-        fwd_act(e, 1)
+    for e in range(n_loc + 1):
+        if e < n_loc:
+            fwd_act(e, 1)
+        if e >= 1:
+            fwd_out(e - 1, 1)
+        if e == n_loc - 3:
+            relay(dy_snd)
+    ya_snd.start()
     out(uc, uc_hbm)
     out(u0, u0_hbm)
-    for k in range(n_ch):
-        for e in range(n_loc):
-            fwd_out(e, 1, k)
-        ya_snd[k].start()
-        if k == 1:
-            relay(dy_snd)
-        if k >= 2:
-            forward_y(k - 2)
 
     dy_snd[2].wait_recv()
     out(dyb, dys_hbm)
     bwd_act_dense(1)
+    gather_dy(1)
+    bwd_act(1)
+    ya_snd.wait_recv()
+    y_acc[srows(2), :] += y_a[...]
+    yc_snd.start()
+    out(y_acc.at[pl.ds(2 * tok + y_rows, tok - y_rows)], fwd_hbm.at[pl.ds(tok, tok - y_rows)])
     out(da0, da0_hbm)
     out(db0, db0_hbm)
-    forward_y(n_ch - 2)
-    gather_dy(1)
-    forward_y(n_ch - 1)
-    for e in range(1, n_loc):
-        bwd_act(e)
+    for e in range(2, n_loc + 1):
+        if e < n_loc:
+            bwd_act(e)
+        if e >= 2:
+            bwd_in(e - 1)
+    bwd_in_dense(1, 3)
+    scatter_dx(3)
+    dxa_snd.start()
+    scatter_dx(1)
+    dxb_snd.start()
     out(dac, dac_hbm)
     out(dbc, dbc_hbm)
-    for k in range(n_ch):
-        for e in range(n_loc):
-            bwd_in(e, k)
-        scatter_dx(1, k)
-        dxa_snd[k].start()
-        scatter_dx(0, k)
-        dxb_snd[k].start()
-        if k >= 1:
-            finish_dx(k - 1)
+    bwd_in_dense(0, 2)
+    scatter_dx(2)
+    scatter_dx(0)
+    dxa_snd.wait_recv()
+    dx_acc[srows(2), :] += dx_a[...]
+    out(slot(dx_acc, 2), fwd_hbm.at[pl.ds(0, tok)])
+    dxb_snd.wait_recv()
+    dx_acc[srows(0), :] += dx_b[...]
+    out(slot(dx_acc, 0), dxo_hbm)
     yb_snd.wait_recv()
-    for k in range(n_ch):
-        yc_snd[k].wait_recv()
-        y_ref[:, dcols[k]] = (y_acc[k, 0:tok, :] + y_b[k] + y_c[k]).astype(BF16)
-    finish_dx(n_ch - 1)
+    yc_snd.wait_recv()
+    y_ref[0:y_rows, :] = y_acc[0:y_rows, :] + y_b[0:y_rows, :] + y_c[...]
+    y_ref[y_rows:, :] = y_acc[y_rows:tok, :] + y_b[y_rows:, :]
     for cp in sends:
         cp.wait_send()
     for cp in outs:
@@ -317,15 +336,15 @@
     n_loc, _, ff = w1.shape
     rows = 4 * tok
     cold = (n_loc - 1) * 2 * cap
-    n_ch = d // DC
     any_spec = pl.BlockSpec(memory_space=pl.ANY)
     vmem_spec = pl.BlockSpec(memory_space=pltpu.VMEM)
     sds = jax.ShapeDtypeStruct
     vm = pltpu.VMEM
-    n_send = 3 + 6 + 1 + 4 * n_ch
+    n_send = 14
+    y_rows = tok * Y_SHARE // 8
     return pl.pallas_call(
-        functools.partial(layer_kernel, n_loc, tok, cap, d, ff),
-        out_shape=(sds((tok, d), BF16), sds((tok, d), F32), sds((tok, d), F32),
+        functools.partial(layer_kernel, n_loc, tok, cap, d, ff, y_rows),
+        out_shape=(sds((tok, d), F32), sds((tok, d), F32), sds((2 * tok - y_rows, d), F32),
                    sds((rows, ff), BF16), sds((rows, ff), BF16), sds((rows, ff), BF16),
                    sds((2, cold, ff), BF16), sds((2, cold, ff), BF16), sds((2, cold, ff), BF16),
                    sds((rows, d), BF16), sds((rows, d), BF16), sds((4, 2, n_loc, tok), F32)),
@@ -335,14 +354,13 @@
             vm((n_loc, d, ff), BF16), vm((n_loc, d, ff), BF16), vm((n_loc, ff, d), BF16),
             vm((rows, ff), F32), vm((rows, ff), F32), vm((2, cold, ff), F32), vm((2, cold, ff), F32),
             vm((rows, d), BF16), vm((rows, d), BF16), vm((cold, d), BF16), vm((2, cold, d), BF16), vm((2 * tok, d), BF16),
-            vm((n_ch, rows, DC), F32), vm((n_ch, rows, DC), F32),
-            vm((n_ch, tok, DC), F32), vm((n_ch, tok, DC), F32), vm((n_ch, tok, DC), F32),
-            vm((n_ch, tok, DC), F32), vm((n_ch, tok, DC), F32),
+            vm((rows, d), F32), vm((rows, d), F32),
+            vm((tok, d), F32), vm((tok, d), F32), vm((y_rows, d), F32), vm((tok, d), F32), vm((tok, d), F32),
             vm((2, 4 * n_loc, tok), F32), vm((rows, 128), F32),
             vm((rows, cold), BF16), vm((2, cold, 2 * tok), BF16), vm((2, cold, 128), F32),
-            vm((rows, ff), BF16), vm((rows, ff), BF16), vm((rows, ff), BF16),
+            vm((2 * cap, ff), BF16), vm((rows, ff), BF16), vm((rows, ff), BF16), vm((rows, ff), BF16),
             vm((2, cold, ff), BF16), vm((2, cold, ff), BF16), vm((2, cold, ff), BF16),
-            pltpu.SemaphoreType.DMA((3, n_loc)), pltpu.SemaphoreType.DMA((2,)), pltpu.SemaphoreType.DMA((8 + 2 * n_ch,)),
+            pltpu.SemaphoreType.DMA((3, n_loc)), pltpu.SemaphoreType.DMA((2,)), pltpu.SemaphoreType.DMA((11,)),
             pltpu.SemaphoreType.DMA((n_send,)), pltpu.SemaphoreType.DMA((n_send,)),
         ],
         compiler_params=pltpu.CompilerParams(collective_id=0, has_side_effects=True, vmem_limit_bytes=67_000_000),
@@ -351,8 +369,8 @@
     )(x, dy, ids, gates, w1, w3, w2)
 
 
-def grad_kernel(n_loc, tok, cap, d, ff, u0_hbm, da0_hbm, db0_hbm, uc_hbm, dac_hbm, dbc_hbm, xs_hbm, dys_hbm, inbox, y_in,
-                gw1_hbm, gw3_hbm, gw2_hbm, y_out, u0, da0, db0, uc, dac, dbc, xs, dys,
+def grad_kernel(n_loc, tok, cap, d, ff, u0_hbm, da0_hbm, db0_hbm, uc_hbm, dac_hbm, dbc_hbm, xs_hbm, dys_hbm, inbox,
+                gw1_hbm, gw3_hbm, gw2_hbm, u0, da0, db0, uc, dac, dbc, xs, dys,
                 xt_a, do_a, ut_a, xt_b, do_b, ut_b, xt0, do0, g1, g3, g2, in_sem, act_sem, out_sem):
     blk = 2 * cap
     x_in = pltpu.make_async_copy(xs_hbm, xs, in_sem.at[0])
@@ -374,9 +392,6 @@
     x_in.start()
     each(act_in(1), "start")
     dy_in.start()
-    each(act_in(2), "start")
-    each(act_in(3), "start")
-    y_out[...] = y_in[...]
 
     def prepare(e, xt, do, ut):
         each(act_in(e), "wait")
@@ -408,6 +423,8 @@
     buf_a, buf_b = (xt_a, do_a, ut_a), (xt_b, do_b, ut_b)
     x_in.wait()
     dy_in.wait()
+    each(act_in(2), "start")
+    each(act_in(3), "start")
     prepare(1, *buf_a)
 
     def pair(j, carry):
@@ -452,10 +469,10 @@
     each(out(1, 0), "wait")
 
 
-def grad_call(u0, da0, db0, uc, dac, dbc, xs, dys, inbox, y, n_loc, cap):
+def grad_call(u0, da0, db0, uc, dac, dbc, xs, dys, inbox, cap):
     rows, ff = u0.shape
     d = xs.shape[1]
-    tok = y.shape[0]
+    n_loc, tok = inbox.shape[2:]
     cold = uc.shape[1]
     sds = jax.ShapeDtypeStruct
     vm = pltpu.VMEM
@@ -464,9 +481,9 @@
     act, cact = vm((rows, ff), BF16), vm((2, cold, ff), BF16)
     return pl.pallas_call(
         functools.partial(grad_kernel, n_loc, tok, cap, d, ff),
-        out_shape=(sds((n_loc, d, ff), BF16), sds((n_loc, d, ff), BF16), sds((n_loc, ff, d), BF16), sds((tok, d), BF16)),
-        in_specs=[any_spec] * 8 + [vmem_spec] * 2,
-        out_specs=(any_spec, any_spec, any_spec, vmem_spec),
+        out_shape=(sds((n_loc, d, ff), BF16), sds((n_loc, d, ff), BF16), sds((n_loc, ff, d), BF16)),
+        in_specs=[any_spec] * 8 + [vmem_spec],
+        out_specs=(any_spec, any_spec, any_spec),
         scratch_shapes=[act, act, act, cact, cact, cact, vm((rows, d), BF16), vm((rows, d), BF16)]
         + [vm((d, 4 * cap), BF16), vm((4 * cap, d), BF16), vm((ff, 4 * cap), BF16)] * 2
         + [vm((d, rows), BF16), vm((rows, d), BF16), vm((2, d, ff), BF16), vm((2, d, ff), BF16), vm((2, ff, d), BF16),
@@ -474,7 +491,7 @@
         compiler_params=pltpu.CompilerParams(vmem_limit_bytes=60_000_000),
         cost_estimate=pl.CostEstimate(flops=2 * rows * d * ff * n_loc * 2, bytes_accessed=34 << 20, transcendentals=0),
         name="moe_grads",
-    )(u0, da0, db0, uc, dac, dbc, xs, dys, inbox, y)
+    )(u0, da0, db0, uc, dac, dbc, xs, dys, inbox)
 
 
 def solution(mesh):
@@ -492,10 +509,11 @@
         assert group_size == 4 and (num_experts // 2) % n_loc == 0 and n_loc == 8 and tok_dev == 2 * cap == 128
 
         def device_fn(x, ids, gates, w1, w3, w2, dy):
-            y, dx_own, dx_fwd, *saved = layer_call(x, dy, ids.T, gates.T, w1, w3, w2, cap)
-            dx_in = lax.ppermute(dx_fwd, "ep", [(0, 2), (1, 3), (2, 0), (3, 1)])
-            gw1, gw3, gw2, y = grad_call(*saved, y, n_loc, cap)
-            return y, (dx_own + dx_in).astype(BF16), gw1, gw3, gw2
+            y_own, dx_own, fwd, *saved = layer_call(x, dy, ids.T, gates.T, w1, w3, w2, cap)
+            came = lax.ppermute(fwd, "ep", [(0, 2), (1, 3), (2, 0), (3, 1)])
+            gw1, gw3, gw2 = grad_call(*saved, cap)
+            y_late = jnp.pad(came[tok_dev:], ((2 * tok_dev - came.shape[0], 0), (0, 0)))
+            return (y_own + y_late).astype(BF16), (dx_own + came[:tok_dev]).astype(BF16), gw1, gw3, gw2
 
         return jax.shard_map(device_fn, mesh=mesh, in_specs=(tok_spec, tok_spec, tok_spec, w_spec, w_spec, w_spec, tok_spec),
                              out_specs=(tok_spec, tok_spec, grad_spec, grad_spec, grad_spec), check_vma=False)(

time: 59.8 us -> 55.8 us (0.933)
  Pallas kernels: 56.7 us -> 53.1 us
  starting transfers between devices: 1.57 us -> 0.89 us
    pallas_call x1, Pallas kernels: 40.2 us -> 37.4 us  [layer_call(): pl.pallas_call(functools.partial(layer_kernel, n_loc, tok, cap, d, ff, y_...]
    pallas_call x1, Pallas kernels: 16.5 us -> 15.7 us  [grad_call(): pl.pallas_call(functools.partial(grad_kernel, n_loc, tok, cap, d, ff), ou...]
    ppermute x1, starting transfers between devices: 1.57 us -> 0.89 us  [device_fn(): came = lax.ppermute(fwd, 'ep', [(0, 2), (1, 3), (2, 0), (3, 1)])]
where the time goes in v1:
time: 55.8 us; the launch traced here: 55.6 us
  Pallas kernels  53.1 us (95%)
  other arithmetic  0.9 us (2%)
  starting transfers between devices  0.89 us (2%)
  between operations  0.68 us (1%)
    pallas_call x1, Pallas kernels, layer_call(): pl.pallas_call(functools.partial(layer_kernel, n_loc, tok, cap, d, ff, y_...  37.4 us
    pallas_call x1, Pallas kernels, grad_call(): pl.pallas_call(functools.partial(grad_kernel, n_loc, tok, cap, d, ff), ou...  15.7 us
  transfers between devices with their start and end apart: 1, of which 0 were waited for; matrix products, arithmetic and copies ran while one was open for 0% of the time, Pallas kernels for 28%

profile of v1, /device:TPU:0, one launch (start us, length us, event | category | flops | bytes accessed | tf_op | source)
XLA Modules:
  0.0 55.6 jit_solution(5520863327916425875)
XLA Ops:
  0.6 37.4 %moe_layer.1 = (f32[128,1024]{1,0:T(8,128)}, f32[128,1024]{1,0:T(8,128)}, f32[160,1024]{1,0:T(8,128)}, bf16[512,512]{1,0:T(8,128)(2,1)}, bf16[512,512]{1,0:T(8,1...) custom-call(bf16[128,1024]{1,0:T(8,128)(2,1)} %x_hbm.1, ...), custom_call_target="tpu_custom_call" | custom-call | flops 17179869184 | bytes 37748736 | tf_op jit(solution)/shard_map/moe_layer/pallas_call | solution.py:345
  38.0 0.9 %collective-permute-start = (f32[160,1024]{1,0:T(8,128)}, f32[160,1024]{1,0:T(8,128)S(1)}, u32[]{:S(2)}, u32[]{:S(2)}) collective-permute-start(f32[160,1024]{1,0:T(8,128)} %get-tuple-element.21), channel_id=1, source_target_pairs={{0,2},{1,3},{2,0},{3,1},{4,6},{5,7},{6,4},{7,5}} | collective-permute-start | bytes 1966088 | tf_op jit(solution)/shard_map/ppermute | solution.py:513
  38.9 0.0 copy-start
  38.9 0.0 copy-start.1
  38.9 15.7 %moe_grads.1 = (bf16[8,1024,512]{2,1,0:T(8,128)(2,1)}, bf16[8,1024,512]{2,1,0:T(8,128)(2,1)}, bf16[8,512,1024]{2,1,0:T(8,128)(2,1)}) custom-call(bf16[512,512]{1,0:T(8,128)(2,1)} %get-tuple-element.23.u0_hbm, bf16[512,512]{1,0:T(8,128)(2,1)} %get-tuple-element.24.da0_hbm, bf16[512,512]{1,0:T(8,128)(2,1)} %get-tuple-element.25.db0_hbm, ...), custom_call_target="tpu_custom_call" | custom-call | flops 8589934592 | bytes 35651584 | tf_op jit(solution)/shard_map/moe_grads/pallas_call | solution.py:482
  54.6 0.0 collective-permute-done
  54.7 0.0 copy-done
  54.7 0.0 copy-done.1
  54.7 0.9 %fusion = (bf16[128,1024]{1,0:T(8,128)(2,1)}, bf16[128,1024]{1,0:T(8,128)(2,1)}) fusion(f32[128,1024]{1,0:T(8,128)S(1)} %copy-done.1, f32[160,1024]{1,0:T(8,128)S(1)} %collective-permute-done, f32[128,1024]{1,0:T(8,128)S(1)} %copy-done, f32[32,1024]{1,0:T(8,128)S(1)} %slice.8), kind=kLoop, calls=%fused_computation.1 | loop fusion | flops 524288 | bytes 2228224 | tf_op jit(solution)/shard_map/convert_element_type | solution.py:516
  (1 shorter events, 0.0 us)
Async XLA Ops:
  38.0 16.6 %collective-permute-start = (f32[160,1024]{1,0:T(8,128)}, f32[160,1024]{1,0:T(8,128)S(1)}, u32[]{:S(2)}, u32[]{:S(2)}) collective-permute-start(f32[160,1024]{1,0:T(8,128)} %get-tuple-element.21), channel_id=1, source_target_pairs={{0,2},{1,3},{2,0},{3,1},{4,6},{5,7},{6,4},{7,5}} | collective-permute-start | bytes 1966088 | tf_op jit(solution)/shard_map/ppermute | solution.py:513
  38.9 15.8 %copy-start = (f32[128,1024]{1,0:T(8,128)S(1)}, f32[128,1024]{1,0:T(8,128)}, u32[]{:S(2)}) copy-start(f32[128,1024]{1,0:T(8,128)} %get-tuple-element.20) | copy-start | bytes 1572868
  38.9 15.8 %copy-start.1 = (f32[128,1024]{1,0:T(8,128)S(1)}, f32[128,1024]{1,0:T(8,128)}, u32[]{:S(2)}) copy-start(f32[128,1024]{1,0:T(8,128)} %get-tuple-element.22) | copy-start | bytes 1572868

commit v2 on v1

--- a/solution.py
+++ b/solution.py
@@ -41,9 +41,9 @@
 
 
 def layer_kernel(n_loc, tok, cap, d, ff, y_rows, x_hbm, dy_hbm, ids_ref, gates_ref, w1_hbm, w3_hbm, w2_hbm,
-                 y_ref, dxo_hbm, fwd_hbm, u0_hbm, da0_hbm, db0_hbm, uc_hbm, dac_hbm, dbc_hbm, xs_hbm, dys_hbm, inbox,
-                 w1, w3, w2, c1_0, c2_0, c1_c, c2_c, xb, dyb, xg, doc, do0, y_acc, dx_acc, y_a, y_b, y_c, dx_a, dx_b,
-                 meta, cols_of, pt, pg, rc, u_last, u0, da0, db0, uc, dac, dbc,
+                 yo_hbm, yr_hbm, dxo_hbm, dxp_hbm, fwd_hbm, u0_hbm, da0_hbm, db0_hbm, uc_hbm, dac_hbm, dbc_hbm, xs_hbm, dys_hbm, inbox,
+                 w1, w3, w2, c1_0, c2_0, c1_c, c2_c, xb, dyb, xg, doc, do0, y_acc, dx_acc, y_a, y_b, dx_a,
+                 meta, cols_of, pt, pg, rc, u0, da0, db0, uc, dac, dbc,
                  w_sem, in_sem, out_sem, send_sem, recv_sem):
     half = 2 * tok
     blk = 2 * cap
@@ -59,8 +59,19 @@
     def load(i, src, dst, e):
         return pltpu.make_async_copy(src.at[e], dst.at[e], w_sem.at[i, e])
 
-    def load_w(e):
-        return [load(i, src, dst, e) for i, (src, dst) in enumerate(((w1_hbm, w1), (w3_hbm, w3), (w2_hbm, w2)))]
+    def load_w(i):
+        up = [load(0, w1_hbm, w1, i), load(1, w3_hbm, w3, i)] if i < n_loc else []
+        return up + ([load(2, w2_hbm, w2, i - 1)] if i else [])
+
+    w_in = [load_w(i) for i in range(n_loc + 1)]
+    ahead = 3
+
+    def wait_w(i):
+        for cp in w_in[i]:
+            cp.wait()
+        if i + ahead <= n_loc:
+            for cp in w_in[i + ahead]:
+                cp.start()
 
     sends = []
 
@@ -85,9 +96,6 @@
     dy_in = pltpu.make_async_copy(dy_hbm, slot(dyb, 0), in_sem.at[1])
     x_in.start()
     dy_in.start()
-    for e in range(3):
-        for cp in load_w(e):
-            cp.start()
 
     expert = lax.broadcasted_iota(jnp.int32, (n_exp, tok), 0)
     gate = jnp.zeros((n_exp, tok), F32)
@@ -104,20 +112,23 @@
     barrier = pltpu.get_barrier_semaphore()
     for dev in (partner, remote, diag):
         pl.semaphore_signal(barrier, inc=1, device_id=(dp, dev), device_id_type=MESH)
+    x_in.wait()
+    dy_in.wait()
+    for i in range(ahead):
+        for cp in w_in[i]:
+            cp.start()
     pl.semaphore_wait(barrier, 3)
 
     m_snd = [send(meta.at[:, pl.ds(dev * n_loc, n_loc)], inbox.at[k + 1], dev) for k, dev in enumerate((partner, remote, diag))]
     x_snd, dy_snd = [[send(slot(b, 0), slot(b, 1), partner), send(slot(b, 0), slot(b, 2), remote),
                       send(slot(b, 2), slot(b, 3), partner)] for b in (xb, dyb)]
-    yb_snd, ya_snd, yc_snd = send(slot(y_acc, 1), y_b, partner), send(slot(y_acc, 3), y_a, partner), send(y_acc.at[pl.ds(2 * tok, y_rows)], y_c, remote)
-    dxa_snd, dxb_snd = send(slot(dx_acc, 3), dx_a, partner), send(slot(dx_acc, 1), dx_b, partner)
+    yb_snd, ya_snd, yc_snd = send(slot(y_acc, 1), y_b, partner), send(slot(y_acc, 3), y_a, partner), send(y_acc.at[pl.ds(2 * tok, y_rows)], yr_hbm, remote)
+    dxa_snd, dxb_snd = send(slot(dx_acc, 3), dx_a, partner), send(slot(dx_acc, 1), dxp_hbm, partner)
 
     for cp in m_snd:
         cp.start()
-    x_in.wait()
     x_snd[1].start()
     x_snd[0].start()
-    dy_in.wait()
     dy_snd[1].start()
     dy_snd[0].start()
 
@@ -134,15 +145,10 @@
         return slice(s * tok, (s + 1) * tok)
 
     def brows(e):
-        if isinstance(e, int):
-            return slice((e - 1) * blk, e * blk)
-        return pl.ds(pl.multiple_of((e - 1) * blk, blk), blk)
+        return slice((e - 1) * blk, e * blk)
 
     def gate_col(e, h):
-        if isinstance(e, int):
-            return cols_of[hrows(h), e:e + 1]
-        lane = lax.broadcasted_iota(jnp.int32, (half, 128), 1)
-        return jnp.sum(jnp.where(lane == e, cols_of[hrows(h), :], 0.0), axis=1, keepdims=True)
+        return cols_of[hrows(h), e:e + 1]
 
     def gather_x(h):
         for c in dcols:
@@ -156,12 +162,11 @@
                 doc[h, r, c] = (g * jnp.dot(pg[h, r, :], dyb[hrows(h), c], preferred_element_type=F32)).astype(BF16)
 
     def fwd_act(e, h):
-        dense = isinstance(e, int) and e == 0
-        x = xb[hrows(h), :] if dense else xg[brows(e), :]
+        x = xb[hrows(h), :] if e == 0 else xg[brows(e), :]
         for c in chunks(ff, 256):
             a = jnp.dot(x, w1[e, :, c], preferred_element_type=F32)
             b = jnp.dot(x, w3[e, :, c], preferred_element_type=F32)
-            if dense:
+            if e == 0:
                 routed = gate_col(e, h) > 0
                 a = jnp.where(routed, a, 0.0)
                 b = jnp.where(routed, b, 0.0)
@@ -169,20 +174,17 @@
             s_a = a * s
             p1 = b * (s + s_a * (1.0 - s))
             u = (s_a * b).astype(BF16)
-            if dense:
+            if e == 0:
                 c1_0[hrows(h), c], c2_0[hrows(h), c], u0[hrows(h), c] = p1, s_a, u
             else:
                 c1_c[h, brows(e), c], c2_c[h, brows(e), c], uc[h, brows(e), c] = p1, s_a, u
-                if h == 0:
-                    u_last[:, c] = u
 
     def fwd_out(e, h):
-        dense = isinstance(e, int) and e == 0
-        u = u0[hrows(h), :] if dense else u_last[...] if h == 0 else uc[h, brows(e), :]
+        u = u0[hrows(h), :] if e == 0 else uc[h, brows(e), :]
         g = gate_col(e, h)
         for c in dcols:
             o = jnp.dot(u, w2[e, :, c], preferred_element_type=F32).astype(BF16)
-            if dense:
+            if e == 0:
                 y_acc[hrows(h), c] = g * o.astype(F32)
             else:
                 y_acc[hrows(h), c] += g * jnp.dot(pt[hrows(h), brows(e)], o, preferred_element_type=F32)
@@ -227,53 +229,38 @@
         for c in dcols:
             dx_acc[srows(s), c] += jnp.dot(pt[srows(s), :], doc[s // 2, :, c], preferred_element_type=F32)
 
+    def export_act(first, last):
+        rows = pl.ds((first - 1) * blk, (last - first + 1) * blk)
+        for src, dst in ((dac, dac_hbm), (dbc, dbc_hbm)):
+            out(src.at[:, rows], dst.at[:, rows])
+
     def relay(snd):
         snd[1].wait_recv()
         snd[2].start()
 
     inbox[0] = meta[:, pl.ds(me * n_loc, n_loc), :]
     build_tables(inbox, cols_of, pt, tok, cap, n_loc, 0)
-    for cp in m_snd:
-        cp.wait_recv()
+    m_snd[0].wait_recv()
     x_snd[0].wait_recv()
-    for e in range(2):
-        for cp in load_w(e):
-            cp.wait()
-        for cp in load_w(e + 3):
-            cp.start()
     build_tables(inbox, cols_of, pt, tok, cap, n_loc, 1)
-    fwd_act(0, 0)
     pickers(0)
     gather_x(0)
-    for s in (2, 3):
-        build_tables(inbox, cols_of, pt, tok, cap, n_loc, s)
-    pickers(1)
-    fwd_act(1, 0)
-    fwd_out(0, 0)
-
-    def own(e, carry):
-        for cp in load_w(e):
-            cp.wait()
-
-        @pl.when(e + 3 < n_loc)
-        def _():
-            for cp in load_w(e + 3):
-                cp.start()
-
-        @pl.when(e == n_loc - 1)
-        def _():
+    for i in range(n_loc + 1):
+        wait_w(i)
+        if i == 2:
+            m_snd[1].wait_recv()
+            m_snd[2].wait_recv()
+        if i == n_loc - 1:
             relay(x_snd)
-
-        fwd_out(e - 1, 0)
-        fwd_act(e, 0)
-        return carry
-
-    lax.fori_loop(2, n_loc, own, 0)
-    dy_snd[0].wait_recv()
-    fwd_out(n_loc - 1, 0)
-    gather_dy(0)
+        if i < n_loc:
+            fwd_act(i, 0)
+        if i == 2:
+            for s in (2, 3):
+                build_tables(inbox, cols_of, pt, tok, cap, n_loc, s)
+            pickers(1)
+        if i >= 1:
+            fwd_out(i - 1, 0)
     yb_snd.start()
-    bwd_act_dense(0)
 
     x_snd[2].wait_recv()
     out(xb, xs_hbm)
@@ -288,43 +275,47 @@
     ya_snd.start()
     out(uc, uc_hbm)
     out(u0, u0_hbm)
+    dy_snd[0].wait_recv()
+    gather_dy(0)
+    bwd_act_dense(0)
 
     dy_snd[2].wait_recv()
+    yb_snd.wait_recv()
     out(dyb, dys_hbm)
-    bwd_act_dense(1)
-    gather_dy(1)
-    bwd_act(1)
+    y_acc[srows(0), :] += y_b[...]
     ya_snd.wait_recv()
     y_acc[srows(2), :] += y_a[...]
     yc_snd.start()
     out(y_acc.at[pl.ds(2 * tok + y_rows, tok - y_rows)], fwd_hbm.at[pl.ds(tok, tok - y_rows)])
+    out(slot(y_acc, 0), yo_hbm)
+    bwd_act_dense(1)
+    gather_dy(1)
     out(da0, da0_hbm)
     out(db0, db0_hbm)
-    for e in range(2, n_loc + 1):
+    bwd_act(1)
+    bwd_act(2)
+    for e in range(3, n_loc + 2):
         if e < n_loc:
             bwd_act(e)
-        if e >= 2:
-            bwd_in(e - 1)
+        if e == 4:
+            export_act(1, 4)
+        if e == n_loc:
+            export_act(5, n_loc - 1)
+        bwd_in(e - 2)
     bwd_in_dense(1, 3)
     scatter_dx(3)
     dxa_snd.start()
     scatter_dx(1)
     dxb_snd.start()
-    out(dac, dac_hbm)
-    out(dbc, dbc_hbm)
     bwd_in_dense(0, 2)
+    scatter_dx(0)
+    out(slot(dx_acc, 0), dxo_hbm)
     scatter_dx(2)
-    scatter_dx(0)
     dxa_snd.wait_recv()
     dx_acc[srows(2), :] += dx_a[...]
     out(slot(dx_acc, 2), fwd_hbm.at[pl.ds(0, tok)])
     dxb_snd.wait_recv()
-    dx_acc[srows(0), :] += dx_b[...]
-    out(slot(dx_acc, 0), dxo_hbm)
-    yb_snd.wait_recv()
     yc_snd.wait_recv()
-    y_ref[0:y_rows, :] = y_acc[0:y_rows, :] + y_b[0:y_rows, :] + y_c[...]
-    y_ref[y_rows:, :] = y_acc[y_rows:tok, :] + y_b[y_rows:, :]
     for cp in sends:
         cp.wait_send()
     for cp in outs:
@@ -344,23 +335,23 @@
     y_rows = tok * Y_SHARE // 8
     return pl.pallas_call(
         functools.partial(layer_kernel, n_loc, tok, cap, d, ff, y_rows),
-        out_shape=(sds((tok, d), F32), sds((tok, d), F32), sds((2 * tok - y_rows, d), F32),
+        out_shape=(sds((tok, d), F32), sds((y_rows, d), F32), sds((tok, d), F32), sds((tok, d), F32), sds((2 * tok - y_rows, d), F32),
                    sds((rows, ff), BF16), sds((rows, ff), BF16), sds((rows, ff), BF16),
                    sds((2, cold, ff), BF16), sds((2, cold, ff), BF16), sds((2, cold, ff), BF16),
                    sds((rows, d), BF16), sds((rows, d), BF16), sds((4, 2, n_loc, tok), F32)),
         in_specs=[any_spec, any_spec, vmem_spec, vmem_spec, any_spec, any_spec, any_spec],
-        out_specs=(vmem_spec,) + (any_spec,) * 10 + (vmem_spec,),
+        out_specs=(any_spec,) * 13 + (vmem_spec,),
         scratch_shapes=[
             vm((n_loc, d, ff), BF16), vm((n_loc, d, ff), BF16), vm((n_loc, ff, d), BF16),
             vm((rows, ff), F32), vm((rows, ff), F32), vm((2, cold, ff), F32), vm((2, cold, ff), F32),
             vm((rows, d), BF16), vm((rows, d), BF16), vm((cold, d), BF16), vm((2, cold, d), BF16), vm((2 * tok, d), BF16),
             vm((rows, d), F32), vm((rows, d), F32),
-            vm((tok, d), F32), vm((tok, d), F32), vm((y_rows, d), F32), vm((tok, d), F32), vm((tok, d), F32),
+            vm((tok, d), F32), vm((tok, d), F32), vm((tok, d), F32),
             vm((2, 4 * n_loc, tok), F32), vm((rows, 128), F32),
             vm((rows, cold), BF16), vm((2, cold, 2 * tok), BF16), vm((2, cold, 128), F32),
-            vm((2 * cap, ff), BF16), vm((rows, ff), BF16), vm((rows, ff), BF16), vm((rows, ff), BF16),
+            vm((rows, ff), BF16), vm((rows, ff), BF16), vm((rows, ff), BF16),
             vm((2, cold, ff), BF16), vm((2, cold, ff), BF16), vm((2, cold, ff), BF16),
-            pltpu.SemaphoreType.DMA((3, n_loc)), pltpu.SemaphoreType.DMA((2,)), pltpu.SemaphoreType.DMA((11,)),
+            pltpu.SemaphoreType.DMA((3, n_loc)), pltpu.SemaphoreType.DMA((2,)), pltpu.SemaphoreType.DMA((14,)),
             pltpu.SemaphoreType.DMA((n_send,)), pltpu.SemaphoreType.DMA((n_send,)),
         ],
         compiler_params=pltpu.CompilerParams(collective_id=0, has_side_effects=True, vmem_limit_bytes=67_000_000),
@@ -509,11 +500,11 @@
         assert group_size == 4 and (num_experts // 2) % n_loc == 0 and n_loc == 8 and tok_dev == 2 * cap == 128
 
         def device_fn(x, ids, gates, w1, w3, w2, dy):
-            y_own, dx_own, fwd, *saved = layer_call(x, dy, ids.T, gates.T, w1, w3, w2, cap)
+            y_own, y_came, dx_own, dx_pair, fwd, *saved = layer_call(x, dy, ids.T, gates.T, w1, w3, w2, cap)
             came = lax.ppermute(fwd, "ep", [(0, 2), (1, 3), (2, 0), (3, 1)])
             gw1, gw3, gw2 = grad_call(*saved, cap)
-            y_late = jnp.pad(came[tok_dev:], ((2 * tok_dev - came.shape[0], 0), (0, 0)))
-            return (y_own + y_late).astype(BF16), (dx_own + came[:tok_dev]).astype(BF16), gw1, gw3, gw2
+            y = y_own + jnp.concatenate([y_came, came[tok_dev:]], axis=0)
+            return y.astype(BF16), (dx_own + dx_pair + came[:tok_dev]).astype(BF16), gw1, gw3, gw2
 
         return jax.shard_map(device_fn, mesh=mesh, in_specs=(tok_spec, tok_spec, tok_spec, w_spec, w_spec, w_spec, tok_spec),
                              out_specs=(tok_spec, tok_spec, grad_spec, grad_spec, grad_spec), check_vma=False)(

time: 55.8 us -> 52.4 us (0.939)
  Pallas kernels: 53.1 us -> 49.6 us
    pallas_call x1, Pallas kernels: 37.4 us -> 33.8 us  [layer_call(): pl.pallas_call(functools.partial(layer_kernel, n_loc, tok, cap, d, ff, y_...]
  transfers between devices with their start and end apart: 1 -> 1, of which waited for: 0 -> 0; matrix products, arithmetic and copies ran while one was open for 0% -> 0% of each run, Pallas kernels for 28% -> 30%
where the time goes in v2:
time: 52.4 us; the launch traced here: 52.2 us
  Pallas kernels  49.6 us (95%)
  other arithmetic  0.97 us (2%)
  starting transfers between devices  0.94 us (2%)
  between operations  0.7 us (1%)
    pallas_call x1, Pallas kernels, layer_call(): pl.pallas_call(functools.partial(layer_kernel, n_loc, tok, cap, d, ff, y_...  33.8 us
    pallas_call x1, Pallas kernels, grad_call(): pl.pallas_call(functools.partial(grad_kernel, n_loc, tok, cap, d, ff), ou...  15.8 us
  transfers between devices with their start and end apart: 1, of which 0 were waited for; matrix products, arithmetic and copies ran while one was open for 0% of the time, Pallas kernels for 30%

profile of v2, /device:TPU:0, one launch (start us, length us, event | category | flops | bytes accessed | tf_op | source)
XLA Modules:
  0.0 52.2 jit_solution(219528042560262168)
XLA Ops:
  0.6 33.8 %moe_layer.1 = (f32[128,1024]{1,0:T(8,128)}, f32[96,1024]{1,0:T(8,128)}, f32[128,1024]{1,0:T(8,128)}, f32[128,1024]{1,0:T(8,128)}, f32[160,1024]{1,0:T(8,128)}, ...) custom-call(bf16[128,1024]{1,0:T(8,128)(2,1)} %x_hbm.1, ...), custom_call_target="tpu_custom_call" | custom-call | flops 17179869184 | bytes 37748736 | tf_op jit(solution)/shard_map/moe_layer/pallas_call | solution.py:336
  34.5 0.9 %collective-permute-start = (f32[160,1024]{1,0:T(8,128)}, f32[160,1024]{1,0:T(8,128)S(1)}, u32[]{:S(2)}, u32[]{:S(2)}) collective-permute-start(f32[160,1024]{1,0:T(8,128)} %get-tuple-element.24), channel_id=1, source_target_pairs={{0,2},{1,3},{2,0},{3,1},{4,6},{5,7},{6,4},{7,5}} | collective-permute-start | bytes 1966088 | tf_op jit(solution)/shard_map/ppermute | solution.py:504
  35.4 0.0 copy-start
  35.4 0.0 copy-start.1
  35.4 0.0 copy-start.2
  35.4 0.0 copy-start.3
  35.4 15.8 %moe_grads.1 = (bf16[8,1024,512]{2,1,0:T(8,128)(2,1)}, bf16[8,1024,512]{2,1,0:T(8,128)(2,1)}, bf16[8,512,1024]{2,1,0:T(8,128)(2,1)}) custom-call(bf16[512,512]{1,0:T(8,128)(2,1)} %get-tuple-element.27.u0_hbm, bf16[512,512]{1,0:T(8,128)(2,1)} %get-tuple-element.28.da0_hbm, bf16[512,512]{1,0:T(8,128)(2,1)} %get-tuple-element.29.db0_hbm, ...), custom_call_target="tpu_custom_call" | custom-call | flops 8589934592 | bytes 35651584 | tf_op jit(solution)/shard_map/moe_grads/pallas_call | solution.py:473
  51.2 0.0 collective-permute-done
  51.2 0.0 copy-done
  51.2 0.0 copy-done.1
  51.2 0.0 copy-done.2
  51.2 0.0 copy-done.3
  51.3 1.0 %fusion = (bf16[128,1024]{1,0:T(8,128)(2,1)}, bf16[128,1024]{1,0:T(8,128)(2,1)}) fusion(f32[160,1024]{1,0:T(8,128)S(1)} %collective-permute-done, f32[128,1024]{1,0:T(8,128)S(1)} %copy-done.1, f32[128,1024]{1,0:T(8,128)S(1)} %copy-done.2, f32[128,1024]{1,0:T(8,128)S(1)} %copy-done, f32[32,1024]{1,0:T(8,128)S(1)} %slice.8, f32[96,1024]{1,0:T(8,128)S(1)} %copy-done.3), kind=kLoop, calls=%fused_computation.1 | loop fusion | flops 786432 | bytes 3145728 | tf_op jit(solution)/shard_map/convert_element_type | solution.py:507
  (1 shorter events, 0.0 us)
Async XLA Ops:
  34.5 16.7 %collective-permute-start = (f32[160,1024]{1,0:T(8,128)}, f32[160,1024]{1,0:T(8,128)S(1)}, u32[]{:S(2)}, u32[]{:S(2)}) collective-permute-start(f32[160,1024]{1,0:T(8,128)} %get-tuple-element.24), channel_id=1, source_target_pairs={{0,2},{1,3},{2,0},{3,1},{4,6},{5,7},{6,4},{7,5}} | collective-permute-start | bytes 1966088 | tf_op jit(solution)/shard_map/ppermute | solution.py:504
  35.4 15.8 %copy-start = (f32[128,1024]{1,0:T(8,128)S(1)}, f32[128,1024]{1,0:T(8,128)}, u32[]{:S(2)}) copy-start(f32[128,1024]{1,0:T(8,128)} %get-tuple-element.22) | copy-start | bytes 1572868
  35.4 15.8 %copy-start.1 = (f32[128,1024]{1,0:T(8,128)S(1)}, f32[128,1024]{1,0:T(8,128)}, u32[]{:S(2)}) copy-start(f32[128,1024]{1,0:T(8,128)} %get-tuple-element.25) | copy-start | bytes 1572868
  35.4 15.8 %copy-start.2 = (f32[128,1024]{1,0:T(8,128)S(1)}, f32[128,1024]{1,0:T(8,128)}, u32[]{:S(2)}) copy-start(f32[128,1024]{1,0:T(8,128)} %get-tuple-element.26) | copy-start | bytes 1572868
  35.4 15.8 %copy-start.3 = (f32[96,1024]{1,0:T(8,128)S(1)}, f32[96,1024]{1,0:T(8,128)}, u32[]{:S(2)}) copy-start(f32[96,1024]{1,0:T(8,128)} %get-tuple-element.23) | copy-start | bytes 1179652

commit v3 on v2

--- a/solution.py
+++ b/solution.py
@@ -64,7 +64,7 @@
         return up + ([load(2, w2_hbm, w2, i - 1)] if i else [])
 
     w_in = [load_w(i) for i in range(n_loc + 1)]
-    ahead = 3
+    ahead = 4
 
     def wait_w(i):
         for cp in w_in[i]:
@@ -122,7 +122,10 @@
     m_snd = [send(meta.at[:, pl.ds(dev * n_loc, n_loc)], inbox.at[k + 1], dev) for k, dev in enumerate((partner, remote, diag))]
     x_snd, dy_snd = [[send(slot(b, 0), slot(b, 1), partner), send(slot(b, 0), slot(b, 2), remote),
                       send(slot(b, 2), slot(b, 3), partner)] for b in (xb, dyb)]
-    yb_snd, ya_snd, yc_snd = send(slot(y_acc, 1), y_b, partner), send(slot(y_acc, 3), y_a, partner), send(y_acc.at[pl.ds(2 * tok, y_rows)], yr_hbm, remote)
+    yb_snd = send(slot(y_acc, 1), y_b, partner)
+    pieces = ((0, tok // 2, tok // 2), (tok // 2, tok // 2, y_rows - tok // 2))
+    ya_snd = [send(y_acc.at[pl.ds(3 * tok + at, n)], y_a.at[pl.ds(at, n)], partner) for at, n, _ in pieces]
+    yc_snd = [send(y_acc.at[pl.ds(2 * tok + at, m)], yr_hbm.at[pl.ds(at, m)], remote) for at, _, m in pieces]
     dxa_snd, dxb_snd = send(slot(dx_acc, 3), dx_a, partner), send(slot(dx_acc, 1), dxp_hbm, partner)
 
     for cp in m_snd:
@@ -234,6 +237,12 @@
         for src, dst in ((dac, dac_hbm), (dbc, dbc_hbm)):
             out(src.at[:, rows], dst.at[:, rows])
 
+    def forward_y(i):
+        at, n, _ = pieces[i]
+        ya_snd[i].wait_recv()
+        y_acc[2 * tok + at:2 * tok + at + n, :] += y_a[at:at + n, :]
+        yc_snd[i].start()
+
     def relay(snd):
         snd[1].wait_recv()
         snd[2].start()
@@ -242,19 +251,25 @@
     build_tables(inbox, cols_of, pt, tok, cap, n_loc, 0)
     m_snd[0].wait_recv()
     x_snd[0].wait_recv()
-    build_tables(inbox, cols_of, pt, tok, cap, n_loc, 1)
-    pickers(0)
-    gather_x(0)
     for i in range(n_loc + 1):
-        wait_w(i)
-        if i == 2:
+        if i == 0:
+            wait_w(0)
+            build_tables(inbox, cols_of, pt, tok, cap, n_loc, 1)
+        if i % 2:
+            wait_w(i)
+            if i + 1 <= n_loc:
+                wait_w(i + 1)
+        if i == 3:
             m_snd[1].wait_recv()
             m_snd[2].wait_recv()
         if i == n_loc - 1:
             relay(x_snd)
         if i < n_loc:
             fwd_act(i, 0)
-        if i == 2:
+        if i == 0:
+            pickers(0)
+            gather_x(0)
+        if i == 3:
             for s in (2, 3):
                 build_tables(inbox, cols_of, pt, tok, cap, n_loc, s)
             pickers(1)
@@ -272,7 +287,8 @@
             fwd_out(e - 1, 1)
         if e == n_loc - 3:
             relay(dy_snd)
-    ya_snd.start()
+    for cp in ya_snd:
+        cp.start()
     out(uc, uc_hbm)
     out(u0, u0_hbm)
     dy_snd[0].wait_recv()
@@ -283,12 +299,11 @@
     yb_snd.wait_recv()
     out(dyb, dys_hbm)
     y_acc[srows(0), :] += y_b[...]
-    ya_snd.wait_recv()
-    y_acc[srows(2), :] += y_a[...]
-    yc_snd.start()
+    forward_y(0)
+    bwd_act_dense(1)
+    forward_y(1)
     out(y_acc.at[pl.ds(2 * tok + y_rows, tok - y_rows)], fwd_hbm.at[pl.ds(tok, tok - y_rows)])
     out(slot(y_acc, 0), yo_hbm)
-    bwd_act_dense(1)
     gather_dy(1)
     out(da0, da0_hbm)
     out(db0, db0_hbm)
@@ -315,7 +330,8 @@
     dx_acc[srows(2), :] += dx_a[...]
     out(slot(dx_acc, 2), fwd_hbm.at[pl.ds(0, tok)])
     dxb_snd.wait_recv()
-    yc_snd.wait_recv()
+    for cp in yc_snd:
+        cp.wait_recv()
     for cp in sends:
         cp.wait_send()
     for cp in outs:
@@ -331,7 +347,7 @@
     vmem_spec = pl.BlockSpec(memory_space=pltpu.VMEM)
     sds = jax.ShapeDtypeStruct
     vm = pltpu.VMEM
-    n_send = 14
+    n_send = 16
     y_rows = tok * Y_SHARE // 8
     return pl.pallas_call(
         functools.partial(layer_kernel, n_loc, tok, cap, d, ff, y_rows),

time: 52.4 us -> 51.8 us (0.989)
  Pallas kernels: 49.6 us -> 48.9 us
    pallas_call x1, Pallas kernels: 33.8 us -> 33.2 us  [layer_call(): pl.pallas_call(functools.partial(layer_kernel, n_loc, tok, cap, d, ff, y_...]
  transfers between devices with their start and end apart: 1 -> 1, of which waited for: 0 -> 0; matrix products, arithmetic and copies ran while one was open for 0% -> 0% of each run, Pallas kernels for 30% -> 31%
where the time goes in v3:
time: 51.8 us; the launch traced here: 51.6 us
  Pallas kernels  48.9 us (94%)
  other arithmetic  0.97 us (2%)
  starting transfers between devices  0.91 us (2%)
  between operations  0.7 us (1%)
    pallas_call x1, Pallas kernels, layer_call(): pl.pallas_call(functools.partial(layer_kernel, n_loc, tok, cap, d, ff, y_...  33.2 us
    pallas_call x1, Pallas kernels, grad_call(): pl.pallas_call(functools.partial(grad_kernel, n_loc, tok, cap, d, ff), ou...  15.8 us
  transfers between devices with their start and end apart: 1, of which 0 were waited for; matrix products, arithmetic and copies ran while one was open for 0% of the time, Pallas kernels for 31%

profile of v3, /device:TPU:0, one launch (start us, length us, event | category | flops | bytes accessed | tf_op | source)
XLA Modules:
  0.0 51.6 jit_solution(10428441207677408891)
XLA Ops:
  0.6 33.2 %moe_layer.1 = (f32[128,1024]{1,0:T(8,128)}, f32[96,1024]{1,0:T(8,128)}, f32[128,1024]{1,0:T(8,128)}, f32[128,1024]{1,0:T(8,128)}, f32[160,1024]{1,0:T(8,128)}, ...) custom-call(bf16[128,1024]{1,0:T(8,128)(2,1)} %x_hbm.1, ...), custom_call_target="tpu_custom_call" | custom-call | flops 17179869184 | bytes 37748736 | tf_op jit(solution)/shard_map/moe_layer/pallas_call | solution.py:352
  33.8 0.9 %collective-permute-start = (f32[160,1024]{1,0:T(8,128)}, f32[160,1024]{1,0:T(8,128)S(1)}, u32[]{:S(2)}, u32[]{:S(2)}) collective-permute-start(f32[160,1024]{1,0:T(8,128)} %get-tuple-element.24), channel_id=1, source_target_pairs={{0,2},{1,3},{2,0},{3,1},{4,6},{5,7},{6,4},{7,5}} | collective-permute-start | bytes 1966088 | tf_op jit(solution)/shard_map/ppermute | solution.py:520
  34.7 0.0 copy-start
  34.7 0.0 copy-start.1
  34.7 0.0 copy-start.2
  34.7 0.0 copy-start.3
  34.7 15.8 %moe_grads.1 = (bf16[8,1024,512]{2,1,0:T(8,128)(2,1)}, bf16[8,1024,512]{2,1,0:T(8,128)(2,1)}, bf16[8,512,1024]{2,1,0:T(8,128)(2,1)}) custom-call(bf16[512,512]{1,0:T(8,128)(2,1)} %get-tuple-element.27.u0_hbm, bf16[512,512]{1,0:T(8,128)(2,1)} %get-tuple-element.28.da0_hbm, bf16[512,512]{1,0:T(8,128)(2,1)} %get-tuple-element.29.db0_hbm, ...), custom_call_target="tpu_custom_call" | custom-call | flops 8589934592 | bytes 35651584 | tf_op jit(solution)/shard_map/moe_grads/pallas_call | solution.py:489
  50.5 0.0 collective-permute-done
  50.5 0.0 copy-done
  50.6 0.0 copy-done.1
  50.6 0.0 copy-done.2
  50.6 0.0 copy-done.3
  50.6 1.0 %fusion = (bf16[128,1024]{1,0:T(8,128)(2,1)}, bf16[128,1024]{1,0:T(8,128)(2,1)}) fusion(f32[160,1024]{1,0:T(8,128)S(1)} %collective-permute-done, f32[128,1024]{1,0:T(8,128)S(1)} %copy-done.1, f32[128,1024]{1,0:T(8,128)S(1)} %copy-done.2, f32[128,1024]{1,0:T(8,128)S(1)} %copy-done, f32[32,1024]{1,0:T(8,128)S(1)} %slice.8, f32[96,1024]{1,0:T(8,128)S(1)} %copy-done.3), kind=kLoop, calls=%fused_computation.1 | loop fusion | flops 786432 | bytes 3145728 | tf_op jit(solution)/shard_map/convert_element_type | solution.py:523
  (1 shorter events, 0.0 us)
Async XLA Ops:
  33.8 16.7 %collective-permute-start = (f32[160,1024]{1,0:T(8,128)}, f32[160,1024]{1,0:T(8,128)S(1)}, u32[]{:S(2)}, u32[]{:S(2)}) collective-permute-start(f32[160,1024]{1,0:T(8,128)} %get-tuple-element.24), channel_id=1, source_target_pairs={{0,2},{1,3},{2,0},{3,1},{4,6},{5,7},{6,4},{7,5}} | collective-permute-start | bytes 1966088 | tf_op jit(solution)/shard_map/ppermute | solution.py:520
  34.7 15.8 %copy-start = (f32[128,1024]{1,0:T(8,128)S(1)}, f32[128,1024]{1,0:T(8,128)}, u32[]{:S(2)}) copy-start(f32[128,1024]{1,0:T(8,128)} %get-tuple-element.22) | copy-start | bytes 1572868
  34.7 15.8 %copy-start.1 = (f32[128,1024]{1,0:T(8,128)S(1)}, f32[128,1024]{1,0:T(8,128)}, u32[]{:S(2)}) copy-start(f32[128,1024]{1,0:T(8,128)} %get-tuple-element.25) | copy-start | bytes 1572868
  34.7 15.9 %copy-start.2 = (f32[128,1024]{1,0:T(8,128)S(1)}, f32[128,1024]{1,0:T(8,128)}, u32[]{:S(2)}) copy-start(f32[128,1024]{1,0:T(8,128)} %get-tuple-element.26) | copy-start | bytes 1572868
  34.7 15.9 %copy-start.3 = (f32[96,1024]{1,0:T(8,128)S(1)}, f32[96,1024]{1,0:T(8,128)}, u32[]{:S(2)}) copy-start(f32[96,1024]{1,0:T(8,128)} %get-tuple-element.23) | copy-start | bytes 1179652

commit v4 on v3

--- a/solution.py
+++ b/solution.py
@@ -471,9 +471,20 @@
     xt0[...] = xs[...].T
     cold(0, n_loc - 1, *buf_a)
     each(out(1, 0), "wait")
-    grads(1, 0, xt0[...], u0[...].T, do0[...], da0[...], db0[...])
+    last = out(1, 0)[:2]
+    for cp, buf, rhs in zip(last, (g1, g3), (da0[...], db0[...])):
+        for c in chunks(ff, 256):
+            buf[1, :, c] = jnp.dot(xt0[...], rhs[:, c], preferred_element_type=F32).astype(BF16)
+        cp.start()
+    ut0 = u0[...].T
+    for i, wide in enumerate(chunks(d, d // 2)):
+        for c in chunks(d // 2, 256):
+            c = slice(wide.start + c.start, wide.start + c.stop)
+            g2[1, :, c] = jnp.dot(ut0, do0[:, c], preferred_element_type=F32).astype(BF16)
+        last.append(pltpu.make_async_copy(g2.at[1, :, wide], gw2_hbm.at[0, :, wide], out_sem.at[1, 2 + i]))
+        last[-1].start()
     each(out(0, 0), "wait")
-    each(out(1, 0), "wait")
+    each(last, "wait")
 
 
 def grad_call(u0, da0, db0, uc, dac, dbc, xs, dys, inbox, cap):
@@ -494,7 +505,7 @@
         scratch_shapes=[act, act, act, cact, cact, cact, vm((rows, d), BF16), vm((rows, d), BF16)]
         + [vm((d, 4 * cap), BF16), vm((4 * cap, d), BF16), vm((ff, 4 * cap), BF16)] * 2
         + [vm((d, rows), BF16), vm((rows, d), BF16), vm((2, d, ff), BF16), vm((2, d, ff), BF16), vm((2, ff, d), BF16),
-           pltpu.SemaphoreType.DMA((5,)), pltpu.SemaphoreType.DMA((3, n_loc)), pltpu.SemaphoreType.DMA((2, 3))],
+           pltpu.SemaphoreType.DMA((5,)), pltpu.SemaphoreType.DMA((3, n_loc)), pltpu.SemaphoreType.DMA((2, 4))],
         compiler_params=pltpu.CompilerParams(vmem_limit_bytes=60_000_000),
         cost_estimate=pl.CostEstimate(flops=2 * rows * d * ff * n_loc * 2, bytes_accessed=34 << 20, transcendentals=0),
         name="moe_grads",

time: 51.8 us -> 51.6 us (level)
  transfers between devices with their start and end apart: 1 -> 1, of which waited for: 0 -> 1; matrix products, arithmetic and copies ran while one was open for 0% -> 0% of each run, Pallas kernels for 31% -> 30%
where the time goes in v4:
time: 51.6 us; the launch traced here: 51.4 us
  Pallas kernels  48.8 us (95%)
  other arithmetic  0.97 us (2%)
  starting transfers between devices  0.91 us (2%)
  between operations  0.69 us (1%)
    pallas_call x1, Pallas kernels, layer_call(): pl.pallas_call(functools.partial(layer_kernel, n_loc, tok, cap, d, ff, y_...  33.2 us
    pallas_call x1, Pallas kernels, grad_call(): pl.pallas_call(functools.partial(grad_kernel, n_loc, tok, cap, d, ff), ou...  15.6 us
  transfers between devices with their start and end apart: 1, of which 1 were waited for; matrix products, arithmetic and copies ran while one was open for 0% of the time, Pallas kernels for 30%

profile of v4, /device:TPU:0, one launch (start us, length us, event | category | flops | bytes accessed | tf_op | source)
XLA Modules:
  0.0 51.4 jit_solution(4465349553067522768)
XLA Ops:
  0.6 33.2 %moe_layer.1 = (f32[128,1024]{1,0:T(8,128)}, f32[96,1024]{1,0:T(8,128)}, f32[128,1024]{1,0:T(8,128)}, f32[128,1024]{1,0:T(8,128)}, f32[160,1024]{1,0:T(8,128)}, ...) custom-call(bf16[128,1024]{1,0:T(8,128)(2,1)} %x_hbm.1, ...), custom_call_target="tpu_custom_call" | custom-call | flops 17179869184 | bytes 37748736 | tf_op jit(solution)/shard_map/moe_layer/pallas_call | solution.py:352
  33.8 0.9 %collective-permute-start = (f32[160,1024]{1,0:T(8,128)}, f32[160,1024]{1,0:T(8,128)S(1)}, u32[]{:S(2)}, u32[]{:S(2)}) collective-permute-start(f32[160,1024]{1,0:T(8,128)} %get-tuple-element.24), channel_id=1, source_target_pairs={{0,2},{1,3},{2,0},{3,1},{4,6},{5,7},{6,4},{7,5}} | collective-permute-start | bytes 1966088 | tf_op jit(solution)/shard_map/ppermute | solution.py:531
  34.7 0.0 copy-start
  34.7 0.0 copy-start.1
  34.7 0.0 copy-start.2
  34.7 0.0 copy-start.3
  34.7 15.6 %moe_grads.1 = (bf16[8,1024,512]{2,1,0:T(8,128)(2,1)}, bf16[8,1024,512]{2,1,0:T(8,128)(2,1)}, bf16[8,512,1024]{2,1,0:T(8,128)(2,1)}) custom-call(bf16[512,512]{1,0:T(8,128)(2,1)} %get-tuple-element.27.u0_hbm, bf16[512,512]{1,0:T(8,128)(2,1)} %get-tuple-element.28.da0_hbm, bf16[512,512]{1,0:T(8,128)(2,1)} %get-tuple-element.29.db0_hbm, ...), custom_call_target="tpu_custom_call" | custom-call | flops 8589934592 | bytes 35651584 | tf_op jit(solution)/shard_map/moe_grads/pallas_call | solution.py:500
  50.4 0.1 collective-permute-done
  50.4 0.0 copy-done
  50.4 0.0 copy-done.1
  50.4 0.0 copy-done.2
  50.5 0.0 copy-done.3
  50.5 1.0 %fusion = (bf16[128,1024]{1,0:T(8,128)(2,1)}, bf16[128,1024]{1,0:T(8,128)(2,1)}) fusion(f32[160,1024]{1,0:T(8,128)S(1)} %collective-permute-done, f32[128,1024]{1,0:T(8,128)S(1)} %copy-done.1, f32[128,1024]{1,0:T(8,128)S(1)} %copy-done.2, f32[128,1024]{1,0:T(8,128)S(1)} %copy-done, f32[32,1024]{1,0:T(8,128)S(1)} %slice.8, f32[96,1024]{1,0:T(8,128)S(1)} %copy-done.3), kind=kLoop, calls=%fused_computation.1 | loop fusion | flops 786432 | bytes 3145728 | tf_op jit(solution)/shard_map/convert_element_type | solution.py:534
  (1 shorter events, 0.0 us)
Async XLA Ops:
  33.8 16.6 %collective-permute-start = (f32[160,1024]{1,0:T(8,128)}, f32[160,1024]{1,0:T(8,128)S(1)}, u32[]{:S(2)}, u32[]{:S(2)}) collective-permute-start(f32[160,1024]{1,0:T(8,128)} %get-tuple-element.24), channel_id=1, source_target_pairs={{0,2},{1,3},{2,0},{3,1},{4,6},{5,7},{6,4},{7,5}} | collective-permute-start | bytes 1966088 | tf_op jit(solution)/shard_map/ppermute | solution.py:531
  34.7 15.7 %copy-start = (f32[128,1024]{1,0:T(8,128)S(1)}, f32[128,1024]{1,0:T(8,128)}, u32[]{:S(2)}) copy-start(f32[128,1024]{1,0:T(8,128)} %get-tuple-element.22) | copy-start | bytes 1572868
  34.7 15.7 %copy-start.1 = (f32[128,1024]{1,0:T(8,128)S(1)}, f32[128,1024]{1,0:T(8,128)}, u32[]{:S(2)}) copy-start(f32[128,1024]{1,0:T(8,128)} %get-tuple-element.25) | copy-start | bytes 1572868
  34.7 15.7 %copy-start.2 = (f32[128,1024]{1,0:T(8,128)S(1)}, f32[128,1024]{1,0:T(8,128)}, u32[]{:S(2)}) copy-start(f32[128,1024]{1,0:T(8,128)} %get-tuple-element.26) | copy-start | bytes 1572868
  34.7 15.7 %copy-start.3 = (f32[96,1024]{1,0:T(8,128)S(1)}, f32[96,1024]{1,0:T(8,128)}, u32[]{:S(2)}) copy-start(f32[96,1024]{1,0:T(8,128)} %get-tuple-element.23) | copy-start | bytes 1179652
